TPU v7x, 16 devices: a whole 2x2x2 slice. The times are simulated.
16 devices in a mesh: dp: 2 (over z), tp: 8 (over y, x, core).
Axes of the slice: x: 2, y: 2, z: 2, core: 2. Of those that a mesh axis runs over, the one named last changes fastest.
Arguments:
- residual: float32 [1024, 1536], P('dp'), parts along dimension 0
- norm_w: bfloat16 [2, 1536], replicated
- w_in: bfloat16 [2, 1536, 2, 3072], P(None, None, None, 'tp')
- conv_w: bfloat16 [2, 4, 3072], P(None, None, 'tp')
- conv_b: bfloat16 [2, 3072], P(None, 'tp')
- w_x: bfloat16 [2, 3072, 128], P(None, 'tp')
- w_dt: bfloat16 [2, 96, 3072], P(None, None, 'tp')
- b_dt: float32 [2, 3072], P(None, 'tp')
- a_log: float32 [2, 16, 3072], P(None, None, 'tp')
- d_skip: float32 [2, 3072], P(None, 'tp')
- w_out: bfloat16 [2, 3072, 1536], P(None, 'tp')
- conv_state: bfloat16 [2, 1024, 3, 3072], P(None, 'dp', None, 'tp'), parts along dimension 1
- ssm_state: float32 [2, 1024, 16, 3072], P(None, 'dp', None, 'tp'), parts along dimension 1
Outputs:
- output 1: float32 [1024, 1536], P('dp'), parts along dimension 0
- output 2: bfloat16 [2, 1024, 3, 3072], P(None, 'dp', None, 'tp'), parts along dimension 1
- output 3: float32 [2, 1024, 16, 3072], P(None, 'dp', None, 'tp'), parts along dimension 1
There are 2 independent parts. A program takes and returns all parts, laid end to end along the dimension named above; an argument that names none is the same for every part.
All inputs are finite; a program needn't handle non-finite values.
Results may differ from a plain program's by a relative error of at most 0.0189318.
Values are sent between devices in bfloat16 or wider.
A program may use at most 1 GiB of HBM per device.

v0:
```python
import jax
import jax.numpy as jnp
from jax import lax
from jax.sharding import PartitionSpec as P


def rms_norm(vector, epsilon):
    return vector * lax.rsqrt(jnp.mean(vector * vector, axis=-1, keepdims=True) + epsilon)


def solution(mesh):
    def device_step(residual, norm_w, w_in, conv_w, conv_b, w_x, w_dt, b_dt, a_log, d_skip, w_out, conv_state, ssm_state):
        rank_dim = w_dt.shape[1]
        state_dim = a_log.shape[1]
        conv_list = []
        ssm_list = []
        for layer_idx in range(norm_w.shape[0]):
            hidden = (rms_norm(residual, 1e-5) * norm_w[layer_idx].astype(jnp.float32)).astype(jnp.bfloat16)
            xz_val = jnp.einsum('bd,dwe->bwe', hidden, w_in[layer_idx], preferred_element_type=jnp.float32).astype(jnp.bfloat16)
            window = jnp.concatenate([conv_state[layer_idx], xz_val[:, 0:1, :]], axis=1)
            conv_pre = jnp.sum(window.astype(jnp.float32) * conv_w[layer_idx].astype(jnp.float32), axis=1) + conv_b[layer_idx].astype(jnp.float32)
            x_conv = jax.nn.silu(conv_pre).astype(jnp.bfloat16)
            proj_part = jnp.dot(x_conv, w_x[layer_idx], preferred_element_type=jnp.float32).astype(jnp.bfloat16)
            proj_sum = lax.psum(proj_part, 'tp').astype(jnp.float32)
            dt_low = rms_norm(proj_sum[:, :rank_dim], 1e-6).astype(jnp.bfloat16)
            b_vec = rms_norm(proj_sum[:, rank_dim:rank_dim + state_dim], 1e-6)
            c_vec = rms_norm(proj_sum[:, rank_dim + state_dim:], 1e-6)
            dt_val = jax.nn.softplus(jnp.dot(dt_low, w_dt[layer_idx], preferred_element_type=jnp.float32) + b_dt[layer_idx])
            x_float = x_conv.astype(jnp.float32)
            decay_fac = jnp.exp(dt_val[:, None, :] * -jnp.exp(a_log[layer_idx]))
            new_ssm = decay_fac * ssm_state[layer_idx] + (dt_val * x_float)[:, None, :] * b_vec[:, :, None]
            y_val = jnp.sum(new_ssm * c_vec[:, :, None], axis=1) + d_skip[layer_idx] * x_float
            gated_y = (y_val * jax.nn.silu(xz_val[:, 1, :].astype(jnp.float32))).astype(jnp.bfloat16)
            out_part = jnp.dot(gated_y, w_out[layer_idx], preferred_element_type=jnp.float32).astype(jnp.bfloat16)
            residual = residual + lax.psum(out_part, 'tp').astype(jnp.float32)
            conv_list.append(window[:, 1:, :])
            ssm_list.append(new_ssm)
        return residual, jnp.stack(conv_list), jnp.stack(ssm_list)

    cache_spec = P(None, 'dp', None, 'tp')
    in_specs = (P('dp', None), P(None, None), P(None, None, None, 'tp'), P(None, None, 'tp'), P(None, 'tp'), P(None, 'tp', None), P(None, None, 'tp'), P(None, 'tp'), P(None, None, 'tp'), P(None, 'tp'), P(None, 'tp', None), cache_spec, cache_spec)
    out_specs = (P('dp', None), cache_spec, cache_spec)
    return jax.shard_map(device_step, mesh=mesh, in_specs=in_specs, out_specs=out_specs, check_vma=False)
```

profile of v0, /device:TPU:0, one launch (start us, length us, event | category | flops | bytes accessed | tf_op | source)
XLA Modules:
  0.0 290.7 jit_solution(1989151288144109054)
XLA Ops:
  7.2 0.0 all-reduce.5.cloned.1.call-start
  7.3 2.3 multiply_reduce_fusion.3
  9.7 0.6 convert_reduce_fusion.1
  10.3 1.2 slice_bitcast_fusion
  11.5 0.9 copy-done.5
  12.4 4.3 %fusion.60 = (bf16[1,1536,2,384]{3,2,1,0:T(2,128)(2,1)S(1)}, bf16[1,1536,2,384]{3,2,1,0:T(2,128)(2,1)}) fusion(bf16[2,1536,2,384]{3,2,1,0:T(2,128)(2,1)S(1)} %copy-done.5), kind=kLoop, calls=%fused_computation.130 | loop fusion | bytes 9437184 | tf_op jit(solution)/shard_map/slice | solution.py:19
  16.7 1.5 fusion.16
  18.2 0.0 copy-start.24
  18.3 0.3 multiply_reduce_fusion.2
  18.6 0.0 copy-start.13
  18.6 0.9 copy-done.13
  19.5 0.2 multiply_convert_fusion.5
  19.7 0.8 copy-done.19
  20.5 0.9 convolution_convert_fusion.3
  21.4 0.0 all-reduce.5.cloned.1.call-update
  21.4 0.0 all-reduce.7.cloned.1.call-start
  21.5 1.4 slice_reduce_fusion.1
  22.9 1.4 negate_bitcast_fusion
  24.2 1.4 slice_reduce_fusion
  25.6 44.5 %all-reduce.5.cloned.1.call-done = bf16[512,128]{1,0:T(8,128)(2,1)} async-done(((bf16[512,128]{1,0:T(8,128)(2,1)}), bf16[512,128]{1,0:T(8,128)(2,1)}) %all-reduce.5.cloned.1.call-update) | async-done | bytes 131088 | tf_op jit(solution)/shard_map/psum | solution.py:24
  70.1 0.9 convert_element_type.133
  71.1 0.1 multiply_reduce_fusion.9
  71.2 0.4 multiply_reduce_fusion.8
  71.6 0.3 slice_multiply_fusion.3
  72.0 1.8 convert_multiply_fusion.3
  73.8 0.0 copy-start.14
  73.8 0.0 copy-start.36
  73.8 11.5 %fusion.5 = f32[512,384]{1,0:T(8,128)S(1)} fusion(f32[2,512,16,384]{3,2,1,0:T(8,128)} %param.25, f32[512,16]{1,0:T(8,128)S(1)} %get-tuple-element.24, f32[512,16]{1,0:T(8,128)S(1)} %get-tuple-element.23, f32[512,384]{1,0:T(8,128)S(1)} %get-tuple-element.29, f32[16,384]{1,0:T(8,128)S(1)} %copy-done.22, f32[512,384]{1,0:T(8,128)S(1)} %get-tuple-element.30), kind=kLoop, calls=%fused_computation.8 | loop fusion | flops 18677760 | bytes 15032320 | tf_op jit(solution)/shard_map/reduce_sum | solution.py:32
  85.5 2.3 convolution_convert_fusion.1
  87.8 0.0 all-reduce.7.cloned.1.call-update
  87.8 0.0 all-reduce.9.cloned.1.call-start
  87.8 2.3 fusion.25
  90.1 48.1 %all-reduce.7.cloned.1.call-done = bf16[512,1536]{1,0:T(8,128)(2,1)} async-done(((bf16[512,1536]{1,0:T(8,128)(2,1)}), bf16[512,1536]{1,0:T(8,128)(2,1)}) %all-reduce.7.cloned.1.call-update) | async-done | bytes 1572880 | tf_op jit(solution)/shard_map/psum | solution.py:35
  138.3 2.0 multiply_reduce_fusion.1
  140.3 0.6 copy-done.18
  140.9 2.4 fusion.19
  143.4 0.0 copy-start.25
  143.4 0.1 fusion.23
  143.6 0.3 multiply_reduce_fusion
  143.9 0.9 copy-done.11
  144.8 0.2 multiply_convert_fusion.3
  145.0 0.7 copy-done.20
  145.8 0.9 convolution_convert_fusion.2
  146.7 0.0 all-reduce.9.cloned.1.call-update
  146.7 0.2 all-reduce.11.cloned.1.call-start
  147.0 1.7 pad_maximum_fusion.1
  148.7 43.2 %all-reduce.9.cloned.1.call-done = bf16[512,128]{1,0:T(8,128)(2,1)} async-done(((bf16[512,128]{1,0:T(8,128)(2,1)}), bf16[512,128]{1,0:T(8,128)(2,1)}) %all-reduce.9.cloned.1.call-update) | async-done | bytes 131088 | tf_op jit(solution)/shard_map/psum | solution.py:24
  191.8 0.9 convert_element_type.148
  192.8 0.1 multiply_reduce_fusion.6
  192.9 0.4 multiply_reduce_fusion.5
  193.3 1.0 slice_multiply_fusion.1
  194.3 3.0 %convert_multiply_fusion.2 = (f32[512,384]{1,0:T(8,128)}, f32[512,384]{1,0:T(8,128)}) fusion(bf16[512,384]{1,0:T(8,128)(2,1)} %copy-done.20, f32[384]{0:T(512)S(1)} %copy-done.34, bf16[2,96,384]{2,1,0:T(8,128)(2,1)} %param.19, f32[512,128]{1,0:T(8,128)S(1)} %convert_element_type.148, f32[512]{0:T(512)S(1)} %add_rsqrt_fusion.2), kind=kOutput, calls=%fused_computation.73 | convolution fusion | flops 39616512 | bytes 2305536 | tf_op jit(solution)/shard_map/dot_general | solution.py:28
  197.4 0.0 slice-start.1
  197.4 0.0 slice-start.2
  197.4 0.0 slice-start.3
  197.4 23.4 %multiply_add_fusion.1 = (f32[1,512,16,384]{3,2,1,0:T(8,128)}, f32[1,512,16,384]{3,2,1,0:T(8,128)}) fusion(f32[2,512,16,384]{3,2,1,0:T(8,128)} %param.25, f32[512,16]{1,0:T(8,128)S(1)} %copy-done.16, f32[512,384]{1,0:T(8,128)S(1)} %copy-done.8, f32[16,384]{1,0:T(8,128)S(1)} %copy-done.23, f32[512,384]{1,0:T(8,128)S(1)} %copy-done.10, ...), kind=kLoop, calls=%fused_computation.10 | loop fusion | flops 25165824 | bytes 53592064 | tf_op jit(solution)/shard_map/add | solution.py:31
  221.0 0.0 copy-start.37
  221.0 6.2 %fusion.2 = f32[512,384]{1,0:T(8,128)S(1)} fusion(f32[2,512,16,384]{3,2,1,0:T(8,128)S(1)} %bitcast.121, f32[512,16]{1,0:T(8,128)} %get-tuple-element.22, f32[512,16]{1,0:T(8,128)S(1)} %get-tuple-element.21, f32[512,384]{1,0:T(8,128)} %get-tuple-element.31, f32[16,384]{1,0:T(8,128)S(1)} %copy-done.21, f32[512,384]{1,0:T(8,128)} %get-tuple-element.32), kind=kLoop, calls=%fused_computation.4 | loop fusion | flops 18677760 | bytes 15032320 | tf_op jit(solution)/shard_map/reduce_sum | solution.py:32
  227.3 2.3 convolution_convert_fusion
  229.5 0.0 all-reduce.11.cloned.1.call-update
  229.6 0.0 copy-start.1
  229.6 17.3 %pad_maximum_fusion = f32[2,512,16,384]{3,2,1,0:T(8,128)} fusion(f32[1,512,16,384]{3,2,1,0:T(8,128)} %get-tuple-element.16, f32[1,512,16,384]{3,2,1,0:T(8,128)} %get-tuple-element.15), kind=kLoop, calls=%fused_computation | loop fusion | flops 6291456 | bytes 50331648 | tf_op jit(solution)/shard_map/stack | solution.py:38
  246.9 33.1 %all-reduce.11.cloned.1.call-done = bf16[512,1536]{1,0:T(8,128)(2,1)} async-done(((bf16[512,1536]{1,0:T(8,128)(2,1)}), bf16[512,1536]{1,0:T(8,128)(2,1)}) %all-reduce.11.cloned.1.call-update) | async-done | bytes 1572880 | tf_op jit(solution)/shard_map/psum | solution.py:35
  280.0 4.1 %convert_add_fusion = f32[512,1536]{1,0:T(8,128)} fusion(bf16[512,1536]{1,0:T(8,128)(2,1)} %all-reduce.11.cloned.1.call-done, f32[512,1536]{1,0:T(8,128)S(1)} %copy-done.1, bf16[512,1536]{1,0:T(8,128)(2,1)} %all-reduce.7.cloned.1.call-done), kind=kLoop, calls=%fused_computation.11 | loop fusion | flops 3145728 | bytes 9437184 | tf_op jit(solution)/shard_map/add | solution.py:35
  (84 shorter events, 0.3 us)
Async XLA Ops:
  7.2 2.4 copy-start.31
  7.2 2.5 copy-start.32
  7.2 2.5 copy-start.30
  7.2 3.1 %copy-start.17 = (bf16[2,512,3,384]{3,1,2,0:T(8,128)(2,1)S(1)}, bf16[2,512,3,384]{3,1,2,0:T(8,128)(2,1)}, u32[]{:S(2)}) copy-start(bf16[2,512,3,384]{3,1,2,0:T(8,128)(2,1)} %param.24) | copy-start | bytes 7077892
  7.2 62.9 %all-reduce.5.cloned.1.call-start = ((), (), s32[]{:S(2)}) async-start(), calls=%async_computation | async-start | bytes 262144 | tf_op jit(solution)/shard_map/psum | solution.py:24
  9.6 2.8 copy-start.5
  12.4 5.8 %copy-start.3 = (bf16[512,3,384]{2,0,1:T(8,128)(2,1)}, bf16[512,3,384]{2,0,1:T(8,128)(2,1)S(1)}, u32[]{:S(2)}) copy-start(bf16[512,3,384]{2,0,1:T(8,128)(2,1)S(1)} %get-tuple-element.20) | copy-start | bytes 3538948
  12.4 4.3 %copy-start = (f32[512,1536]{1,0:T(8,128)S(1)}, f32[512,1536]{1,0:T(8,128)}, u32[]{:S(2)}) copy-start(f32[512,1536]{1,0:T(8,128)} %param.13) | copy-start | bytes 9437188
  18.2 1.5 copy-start.28
  18.2 2.3 copy-start.24
  18.6 0.9 copy-start.13
  19.7 0.8 copy-start.19
  21.4 116.9 %all-reduce.7.cloned.1.call-start = ((), (), s32[]{:S(2)}) async-start(), calls=%async_computation.1 | async-start | bytes 3145728 | tf_op jit(solution)/shard_map/psum | solution.py:35
  70.1 3.6 %copy-start.22 = (f32[16,384]{1,0:T(8,128)S(1)}, f32[16,384]{1,0:T(8,128)}, u32[]{:S(2)}) copy-start(f32[16,384]{1,0:T(8,128)} %get-tuple-element.26) | copy-start | bytes 73732
  72.0 13.4 %copy-start.15 = (f32[512,16]{1,0:T(8,128)}, f32[512,16]{1,0:T(8,128)S(1)}, u32[]{:S(2)}) copy-start(f32[512,16]{1,0:T(8,128)S(1)} %get-tuple-element.23) | copy-start | bytes 98308
  73.8 11.6 %copy-start.7 = (f32[512,384]{1,0:T(8,128)}, f32[512,384]{1,0:T(8,128)S(1)}, u32[]{:S(2)}) copy-start(f32[512,384]{1,0:T(8,128)S(1)} %get-tuple-element.29) | copy-start | bytes 2359300
  73.8 11.6 %copy-start.9 = (f32[512,384]{1,0:T(8,128)}, f32[512,384]{1,0:T(8,128)S(1)}, u32[]{:S(2)}) copy-start(f32[512,384]{1,0:T(8,128)S(1)} %get-tuple-element.30) | copy-start | bytes 2359300
  73.8 11.6 %copy-start.14 = (f32[512,384]{1,0:T(8,128)S(1)}, f32[512,384]{1,0:T(8,128)}, u32[]{:S(2)}) copy-start(f32[512,384]{1,0:T(8,128)} %copy-done.13) | copy-start | bytes 2359300
  73.8 11.6 %copy-start.29 = (bf16[512,2,384]{2,0,1:T(8,128)(2,1)S(1)}, bf16[512,2,384]{2,0,1:T(8,128)(2,1)}, u32[]{:S(2)}) copy-start(bf16[512,2,384]{2,0,1:T(8,128)(2,1)} %copy-done.28) | copy-start | bytes 2359300
  73.8 11.6 %copy-start.35 = (f32[384]{0:T(512)S(1)}, f32[384]{0:T(512)}, u32[]{:S(2)}) copy-start(f32[384]{0:T(512)} %get-tuple-element.10) | copy-start | bytes 4612
  73.8 11.6 %copy-start.36 = (bf16[2,384,1536]{2,1,0:T(8,128)(2,1)S(1)}, bf16[2,384,1536]{2,1,0:T(8,128)(2,1)}, u32[]{:S(2)}) copy-start(bf16[2,384,1536]{2,1,0:T(8,128)(2,1)} %param.23) | copy-start | bytes 7077892
  87.8 104.0 %all-reduce.9.cloned.1.call-start = ((), (), s32[]{:S(2)}) async-start(), calls=%async_computation.2 | async-start | bytes 262144 | tf_op jit(solution)/shard_map/psum | solution.py:24
  138.3 2.1 copy-start.4
  138.3 2.6 copy-start.18
  140.9 2.5 copy-start.2
  143.3 1.7 copy-start.26
  143.4 2.4 copy-start.25
  143.4 3.6 %copy-start.6 = (bf16[1,512,3,384]{3,1,2,0:T(8,128)(2,1)S(1)}, bf16[1,512,3,384]{3,1,2,0:T(8,128)(2,1)}, u32[]{:S(2)}) copy-start(bf16[1,512,3,384]{3,1,2,0:T(8,128)(2,1)} %fusion.25) | copy-start | bytes 3538948
  143.9 0.9 copy-start.11
  145.0 0.8 copy-start.20
  146.7 47.6 %copy-start.34 = (f32[384]{0:T(512)S(1)}, f32[384]{0:T(512)}, u32[]{:S(2)}) copy-start(f32[384]{0:T(512)} %get-tuple-element.11) | copy-start | bytes 4612
  146.7 133.3 %all-reduce.11.cloned.1.call-start = ((), (), s32[]{:S(2)}) async-start(), calls=%async_computation.3 | async-start | bytes 3145728 | tf_op jit(solution)/shard_map/psum | solution.py:35
  148.7 48.7 %copy-start.8 = (f32[512,384]{1,0:T(8,128)S(1)}, f32[512,384]{1,0:T(8,128)}, u32[]{:S(2)}) copy-start(f32[512,384]{1,0:T(8,128)} %copy-done.7) | copy-start | bytes 2359300
  148.7 48.7 %copy-start.10 = (f32[512,384]{1,0:T(8,128)S(1)}, f32[512,384]{1,0:T(8,128)}, u32[]{:S(2)}) copy-start(f32[512,384]{1,0:T(8,128)} %copy-done.9) | copy-start | bytes 2359300
  148.7 48.7 %copy-start.16 = (f32[512,16]{1,0:T(8,128)S(1)}, f32[512,16]{1,0:T(8,128)}, u32[]{:S(2)}) copy-start(f32[512,16]{1,0:T(8,128)} %copy-done.15) | copy-start | bytes 98308
  148.7 48.7 %copy-start.21 = (f32[16,384]{1,0:T(8,128)S(1)}, f32[16,384]{1,0:T(8,128)}, u32[]{:S(2)}) copy-start(f32[16,384]{1,0:T(8,128)} %get-tuple-element.25) | copy-start | bytes 73732
  148.7 48.7 %copy-start.23 = (f32[16,384]{1,0:T(8,128)S(1)}, f32[16,384]{1,0:T(8,128)}, u32[]{:S(2)}) copy-start(f32[16,384]{1,0:T(8,128)} %get-tuple-element.26) | copy-start | bytes 73732
  194.3 26.5 %slice-start = ((s8[25165824]{0:T(1024)(128)(4,1)}), s8[4194304]{0:T(1024)(128)(4,1)S(1)}, s32[]{:S(2)}) async-start(s8[25165824]{0:T(1024)(128)(4,1)} %bitcast.120), calls=%async_computation.4 | async-start | bytes 8388608
  197.4 23.5 %slice-start.1 = ((s8[25165824]{0:T(1024)(128)(4,1)}), s8[4194304]{0:T(1024)(128)(4,1)S(1)}, s32[]{:S(2)}) async-start(s8[25165824]{0:T(1024)(128)(4,1)} %bitcast.120), calls=%async_computation.5 | async-start | bytes 8388608
  197.4 23.5 %slice-start.2 = ((s8[25165824]{0:T(1024)(128)(4,1)}), s8[4194304]{0:T(1024)(128)(4,1)S(1)}, s32[]{:S(2)}) async-start(s8[25165824]{0:T(1024)(128)(4,1)} %bitcast.120), calls=%async_computation.6 | async-start | bytes 8388608
  197.4 23.5 %slice-start.3 = ((s8[25165824]{0:T(1024)(128)(4,1)}), s8[4194304]{0:T(1024)(128)(4,1)S(1)}, s32[]{:S(2)}) async-start(s8[25165824]{0:T(1024)(128)(4,1)} %bitcast.120), calls=%async_computation.7 | async-start | bytes 8388608
  197.4 23.5 %slice-start.4 = ((s8[25165824]{0:T(1024)(128)(4,1)}), s8[4194304]{0:T(1024)(128)(4,1)S(1)}, s32[]{:S(2)}) async-start(s8[25165824]{0:T(1024)(128)(4,1)} %bitcast.120), calls=%async_computation.8 | async-start | bytes 8388608
  197.4 23.5 %slice-start.5 = ((s8[25165824]{0:T(1024)(128)(4,1)}), s8[4194304]{0:T(1024)(128)(4,1)S(1)}, s32[]{:S(2)}) async-start(s8[25165824]{0:T(1024)(128)(4,1)} %bitcast.120), calls=%async_computation.9 | async-start | bytes 8388608
  220.9 6.3 %copy-start.12 = (f32[512,384]{1,0:T(8,128)S(1)}, f32[512,384]{1,0:T(8,128)}, u32[]{:S(2)}) copy-start(f32[512,384]{1,0:T(8,128)} %copy-done.11) | copy-start | bytes 2359300
  220.9 6.3 %copy-start.27 = (bf16[512,2,384]{2,0,1:T(8,128)(2,1)S(1)}, bf16[512,2,384]{2,0,1:T(8,128)(2,1)}, u32[]{:S(2)}) copy-start(bf16[512,2,384]{2,0,1:T(8,128)(2,1)} %copy-done.26) | copy-start | bytes 2359300
  221.0 6.3 %copy-start.33 = (f32[384]{0:T(512)S(1)}, f32[384]{0:T(512)}, u32[]{:S(2)}) copy-start(f32[384]{0:T(512)} %get-tuple-element.9) | copy-start | bytes 4612
  221.0 6.3 %copy-start.37 = (bf16[2,384,1536]{2,1,0:T(8,128)(2,1)S(1)}, bf16[2,384,1536]{2,1,0:T(8,128)(2,1)}, u32[]{:S(2)}) copy-start(bf16[2,384,1536]{2,1,0:T(8,128)(2,1)} %param.23) | copy-start | bytes 7077892
  229.6 50.5 %copy-start.1 = (f32[512,1536]{1,0:T(8,128)S(1)}, f32[512,1536]{1,0:T(8,128)}, u32[]{:S(2)}) copy-start(f32[512,1536]{1,0:T(8,128)} %param.13) | copy-start | bytes 9437188
Sparse Core Ops, SparseCore 0:
  21.5 48.5 all-reduce.4
  87.9 50.3 all-reduce.6
  146.9 44.9 all-reduce.8
  229.7 50.2 all-reduce.10
where the time goes:
time: 291 us
  waiting for transfers between devices  169 us (58%)
  other arithmetic  78.5 us (27%)
  matrix products  15.2 us (5%)
  between operations  14.4 us (5%)
  local copies, waits for them, and re-layouts  13.2 us (5%)
    psum x2, waiting for transfers between devices, device_step(): proj_sum = lax.psum(proj_part, 'tp').astype(jnp.float32)  87.7 us
    psum x2, waiting for transfers between devices, device_step(): residual = residual + lax.psum(out_part, 'tp').astype(jnp.float32)  81.3 us
    add x1, other arithmetic, device_step(): decay_fac * ssm_state[layer_idx]  23.4 us
    another operation x4, other arithmetic, device_step(): return (residual, jnp.stack(conv_list), jnp.stack(ssm_list))  21.4 us
    reduce_sum x2, other arithmetic, device_step(): jnp.sum(new_ssm * c_vec[:, :, None], axis=1) + d_skip[layer_idx] * x_float  17.8 us
  transfers between devices with their start and end apart: 4, of which 4 were waited for; matrix products, arithmetic and copies ran while one was open for 9% of the time, Pallas kernels for 0%

commit v1 on v0

v1 whole, which is shorter than its diff:
```python
import functools

import jax
import jax.numpy as jnp
from jax import lax
from jax.experimental import pallas as pl
from jax.experimental.pallas import tpu as pltpu
from jax.sharding import PartitionSpec as P

MESH = pl.DeviceIdType.MESH
LOG2E = 1.4426950408889634
CHUNKS = 4
COPIES = 8


def rms_scale(vector, epsilon):
    return lax.rsqrt(jnp.mean(vector * vector, axis=-1, keepdims=True) + epsilon)


def mamba_kernel(
    residual, w_in, w_out, conv_state, ssm_state, norm_w, conv_w, conv_b, w_x, w_dt, b_dt, a_log, d_skip,
    r_out, conv_out, ssm0, ssm1,
    res, w_raw, w_xz, wo, conv_old, wdt_pad, hid, xc_buf, z_buf, part, half_in, quart_in, own_in, o_acc,
    p_acc, p_send, p_recv, dt_buf, dx_buf, y_part, yg_buf, send_sem, recv_sem, load_sem, state_sem,
):
    layers = 2
    tokens, width = res.shape
    chunk = tokens // CHUNKS
    own = chunk // 8
    inner = wo.shape[1]
    rank = w_dt.shape[1]
    state = a_log.shape[1]
    lane_tiles = inner // 128
    ssm_bufs = (ssm0, ssm1)

    tp = lax.axis_index("tp")
    core = lax.rem(tp, 2)
    pos_x = lax.rem(lax.div(tp, 2), 2)
    pos_y = lax.div(tp, 4)
    bit_a = pos_x * (1 - core) + pos_y * core
    bit_b = pos_y * (1 - core) + pos_x * core
    peer_c = tp + 1 - 2 * core
    peer_a = tp + (1 - 2 * bit_a) * (2 + 2 * core)
    peer_b = tp + (1 - 2 * bit_b) * (4 - 2 * core)

    def rows_of(q):
        return pl.ds(pl.multiple_of(q * chunk, chunk), chunk)

    half_base = core * (4 * own)
    quart_base = half_base + bit_a * (2 * own)
    own_base = quart_base + bit_b * own

    def part_rows(q, base, count):
        return pl.ds(pl.multiple_of(q * chunk + base, own), count)

    def remote(kind, layer, q, src, dst, peer):
        return pltpu.make_async_remote_copy(
            src_ref=src, dst_ref=dst, send_sem=send_sem.at[kind, layer, q], recv_sem=recv_sem.at[kind, layer, q],
            device_id={"tp": peer}, device_id_type=MESH,
        )

    def p_copy(step, layer, q):
        peer = (peer_c, peer_a, peer_b)[step]
        return remote(step, layer, q, p_send.at[step, rows_of(q)], p_recv.at[step, rows_of(q)], peer)

    def o_copy(step, layer, q):
        if step == 0:
            src = part.at[part_rows(q, (1 - core) * (4 * own), 4 * own)]
            return remote(3, layer, q, src, half_in.at[q], peer_c)
        if step == 1:
            src = part.at[part_rows(q, half_base + (1 - bit_a) * (2 * own), 2 * own)]
            return remote(4, layer, q, src, quart_in.at[q], peer_a)
        src = part.at[part_rows(q, quart_base + (1 - bit_b) * own, own)]
        return remote(5, layer, q, src, own_in.at[q], peer_b)

    def h_copy(step, layer, q):
        base, count, peer = ((own_base, own, peer_b), (quart_base, 2 * own, peer_a), (half_base, 4 * own, peer_c))[step]
        ref = hid.at[part_rows(q, base, count)]
        if step == 0:
            return remote(6, layer, q, ref, ref, peer)
        if step == 1:
            return remote(7, layer, q, ref, ref, peer)
        return remote(2 + 6, layer, q, ref, ref, peer)

    def w_load(layer, tile):
        return pltpu.make_async_copy(w_in.at[layer, :, tile], w_raw.at[tile], load_sem.at[tile])

    def res_load(q):
        return pltpu.make_async_copy(residual.at[rows_of(q)], res.at[rows_of(q)], load_sem.at[4 + q])

    def wo_load(layer):
        return pltpu.make_async_copy(w_out.at[layer], wo.at[layer], load_sem.at[10 + layer])

    def conv_load(layer, row):
        dst = conv_old.at[layer] if row == 0 else conv_out.at[layer, row - 1]
        return pltpu.make_async_copy(conv_state.at[layer, row], dst, load_sem.at[12 + 3 * layer + row])

    def state_load(layer, q):
        return pltpu.make_async_copy(ssm_state.at[layer, rows_of(q)], ssm_bufs[layer].at[rows_of(q)], state_sem.at[layer, q])

    for tile in range(lane_tiles):
        w_load(0, tile).start()
    for q in range(CHUNKS):
        res_load(q).start()
    for row in range(3):
        conv_load(0, row).start()

    barrier = pltpu.get_barrier_semaphore()
    for peer in (peer_c, peer_a, peer_b):
        pl.semaphore_signal(barrier, inc=1, device_id={"tp": peer}, device_id_type=MESH)

    for layer in range(layers):
        wdt_pad[layer, :rank] = w_dt[layer]
        wdt_pad[layer, rank:] = jnp.zeros((128 - rank, inner), jnp.bfloat16)

    def split_weights(layer, block):
        row = lax.broadcasted_iota(jnp.int32, (256, 256), 0)
        col = lax.broadcasted_iota(jnp.int32, (256, 256), 1)
        want = jnp.where(row < 128, 2 * row, 2 * row - 255)
        pick = jnp.where(col == want, 1.0, 0.0).astype(jnp.bfloat16)
        raw = [w_raw.at[tile].reshape(2 * width, 128)[pl.ds(pl.multiple_of(block * 256, 256), 256), :] for tile in range(lane_tiles)]
        both = jnp.dot(pick, jnp.concatenate(raw, axis=1), preferred_element_type=jnp.float32).astype(jnp.bfloat16)
        dst = pl.ds(pl.multiple_of(block * 128, 128), 128)
        w_xz[layer, dst, :inner] = both[:128]
        w_xz[layer, dst, inner:] = both[128:]

    blocks = width // 128
    for tile in range(lane_tiles):
        w_load(0, tile).wait()

    @pl.loop(0, blocks)
    def _(block):
        split_weights(0, block)

    for q in range(CHUNKS):
        state_load(0, q).start()
    wo_load(0).start()
    for tile in range(lane_tiles):
        w_load(1, tile).start()
    for row in range(3):
        conv_load(1, row).start()
    wo_load(1).start()
    for row in range(3):
        conv_load(0, row).wait()
    pl.semaphore_wait(barrier, 3)

    def stage_in(layer, q):
        rows = rows_of(q)
        if layer == 0:
            res_load(q).wait()

            @pl.loop(0, chunk // 16)
            def _(i):
                sub = pl.ds(pl.multiple_of(q * chunk + i * 16, 16), 16)
                r = res[sub, :]
                hid[sub, :] = (r * rms_scale(r, 1e-5) * norm_w[0:1, :].astype(jnp.float32)).astype(jnp.bfloat16)
        else:
            h_copy(2, layer - 1, q).wait()
        xz = jnp.dot(hid[rows, :], w_xz[layer], preferred_element_type=jnp.float32)
        x_val = xz[:, :inner].astype(jnp.bfloat16)
        z_buf[rows, :] = xz[:, inner:].astype(jnp.bfloat16)
        conv_out[layer, 2, rows, :] = x_val
        taps = conv_w[layer].astype(jnp.float32)
        pre = conv_old[layer, rows, :].astype(jnp.float32) * taps[0:1]
        pre = pre + conv_out[layer, 0, rows, :].astype(jnp.float32) * taps[1:2]
        pre = pre + conv_out[layer, 1, rows, :].astype(jnp.float32) * taps[2:3]
        pre = pre + x_val.astype(jnp.float32) * taps[3:4]
        pre = pre + conv_b[layer:layer + 1, :].astype(jnp.float32)
        xc = (pre * jax.nn.sigmoid(pre)).astype(jnp.bfloat16)
        xc_buf[rows, :] = xc
        p = jnp.dot(xc, w_x[layer], preferred_element_type=jnp.float32)
        p_acc[rows, :] = p
        p_send[0, rows, :] = p.astype(jnp.bfloat16)
        p_copy(0, layer, q).start()

    def stage_p(step, layer, q):
        rows = rows_of(q)
        p_copy(step - 1, layer, q).wait()
        p = p_acc[rows, :] + p_recv[step - 1, rows, :].astype(jnp.float32)
        p_acc[rows, :] = p
        p_send[step, rows, :] = p.astype(jnp.bfloat16)
        p_copy(step, layer, q).start()

    def stage_ssm(layer, q):
        rows = rows_of(q)
        state_buf = ssm_bufs[layer]
        p_copy(2, layer, q).wait()
        p = p_acc[rows, :] + p_recv[2, rows, :].astype(jnp.float32)
        lane = lax.broadcasted_iota(jnp.int32, p.shape, 1)
        square = p * p
        is_dt = lane < rank
        is_b = jnp.logical_and(lane >= rank, lane < rank + state)

        def scale_of(mask, count):
            total = jnp.sum(jnp.where(mask, square, 0.0), axis=1, keepdims=True)
            return lax.rsqrt(total * (1.0 / count) + 1e-6)

        scale_dt = scale_of(is_dt, rank)
        scale_b = scale_of(is_b, state)
        scale_c = scale_of(lane >= rank + state, state)
        normed = p * jnp.where(is_dt, scale_dt, jnp.where(is_b, scale_b, scale_c))
        dt_low = jnp.where(is_dt, normed, 0.0).astype(jnp.bfloat16)
        pre = jnp.dot(dt_low, wdt_pad[layer], preferred_element_type=jnp.float32) + b_dt[layer:layer + 1, :]
        dt = jnp.maximum(pre, 0.0) + jnp.log1p(jnp.exp(-jnp.abs(pre)))
        dt_buf[...] = dt
        dx_buf[...] = dt * xc_buf[rows, :].astype(jnp.float32)
        turned = normed.T
        b_cols = turned[rank:rank + state, :]
        c_cols = turned[rank + state:, :]
        decay_rate = jnp.exp(a_log[layer]) * (-LOG2E)
        state_load(layer, q).wait()
        group = 8

        def scan_group(g, carry):
            b_now, c_now = carry
            for j in range(group):
                token = g * group + j
                dt_row = dt_buf[pl.ds(token, 1), :]
                dx_row = dx_buf[pl.ds(token, 1), :]
                old = state_buf[q * chunk + token]
                new = jnp.exp2(dt_row * decay_rate) * old + dx_row * b_now[:, j:j + 1]
                state_buf[q * chunk + token] = new
                weighted = new * c_now[:, j:j + 1]
                partial = weighted[:8] + weighted[8:]
                for tile in range(lane_tiles):
                    y_part[tile, pl.ds(pl.multiple_of(token * 8, 8), 8), :] = partial[:, tile * 128:(tile + 1) * 128]
            return pltpu.roll(b_now, chunk - group, 1), pltpu.roll(c_now, chunk - group, 1)

        lax.fori_loop(0, chunk // group, scan_group, (b_cols, c_cols))

        @pl.loop(0, chunk // 16)
        def _(g):
            ys = []
            for k in range(2):
                first = g * 128 + k * 64
                by_tile = []
                for tile in range(lane_tiles):
                    total = y_part[tile, pl.ds(first, 8, stride=8), :]
                    for sub in range(1, 8):
                        total = total + y_part[tile, pl.ds(first + sub, 8, stride=8), :]
                    by_tile.append(total)
                ys.append(jnp.concatenate(by_tile, axis=1))
            sub_rows = pl.ds(pl.multiple_of(q * chunk + g * 16, 16), 16)
            y = jnp.concatenate(ys, axis=0) + d_skip[layer:layer + 1, :] * xc_buf[sub_rows, :].astype(jnp.float32)
            z = z_buf[sub_rows, :].astype(jnp.float32)
            yg_buf[pl.ds(pl.multiple_of(g * 16, 16), 16), :] = (y * (z * jax.nn.sigmoid(z))).astype(jnp.bfloat16)

        part[rows, :] = jnp.dot(yg_buf[...], wo[layer], preferred_element_type=jnp.float32).astype(jnp.bfloat16)
        o_copy(0, layer, q).start()

    def stage_sum_half(layer, q):
        o_copy(0, layer, q).wait()
        mine = part_rows(q, half_base, 4 * own)
        part[mine, :] = (part[mine, :].astype(jnp.float32) + half_in[q].astype(jnp.float32)).astype(jnp.bfloat16)
        o_copy(1, layer, q).start()

    def stage_sum_quart(layer, q):
        o_copy(1, layer, q).wait()
        mine = part_rows(q, quart_base, 2 * own)
        part[mine, :] = (part[mine, :].astype(jnp.float32) + quart_in[q].astype(jnp.float32)).astype(jnp.bfloat16)
        o_copy(2, layer, q).start()

    def stage_own(layer, q):
        o_copy(2, layer, q).wait()
        mine = part_rows(q, own_base, own)
        o_val = part[mine, :].astype(jnp.float32) + own_in[q].astype(jnp.float32)
        if layer == 0:
            o_acc[q] = o_val
            r = res[mine, :] + o_val
            hid[mine, :] = (r * rms_scale(r, 1e-5) * norm_w[1:2, :].astype(jnp.float32)).astype(jnp.bfloat16)
        else:
            hid[mine, :] = (o_acc[q] + o_val).astype(jnp.bfloat16)
        h_copy(0, layer, q).start()

    def stage_gather(step, layer, q):
        h_copy(step - 1, layer, q).wait()
        h_copy(step, layer, q).start()

    def stage_out(q):
        h_copy(2, layers - 1, q).wait()
        rows = rows_of(q)
        r_out[rows, :] = res[rows, :] + hid[rows, :].astype(jnp.float32)

    stages = []
    for layer in range(layers):
        stages.append(functools.partial(stage_in, layer))
        stages.append(functools.partial(stage_p, 1, layer))
        stages.append(functools.partial(stage_p, 2, layer))
        stages.append(functools.partial(stage_ssm, layer))
        stages.append(functools.partial(stage_sum_half, layer))
        stages.append(functools.partial(stage_sum_quart, layer))
        stages.append(functools.partial(stage_own, layer))
        stages.append(functools.partial(stage_gather, 1, layer))
        stages.append(functools.partial(stage_gather, 2, layer))
    stages.append(stage_out)

    def late_loads(tick):
        @pl.when(tick == 3)
        def _():
            wo_load(0).wait()

        @pl.when(tick == 4)
        def _():
            for tile in range(lane_tiles):
                w_load(1, tile).wait()
            for row in range(3):
                conv_load(1, row).wait()
            wo_load(1).wait()
            for q in range(CHUNKS):
                state_load(1, q).start()

        @pl.when(jnp.logical_and(tick >= 5, tick < 9))
        def _():
            for i in range(blocks // 4):
                split_weights(1, (tick - 5) * (blocks // 4) + i)

    @pl.loop(0, len(stages) + CHUNKS - 1)
    def _(tick):
        late_loads(tick)
        for index in reversed(range(len(stages))):
            q = tick - index

            @pl.when(jnp.logical_and(q >= 0, q < CHUNKS))
            def _():
                stages[index](q)


def dump_kernel(r_val, conv_val, ssm0, ssm1, r_hbm, conv_hbm, ssm_hbm, sems):
    copies = [
        pltpu.make_async_copy(ssm0, ssm_hbm.at[0], sems.at[0]),
        pltpu.make_async_copy(ssm1, ssm_hbm.at[1], sems.at[1]),
        pltpu.make_async_copy(conv_val, conv_hbm, sems.at[2]),
        pltpu.make_async_copy(r_val, r_hbm, sems.at[3]),
    ]
    for copy in copies:
        copy.start()
    for copy in copies:
        copy.wait()


def solution(mesh):
    def device_step(residual, norm_w, w_in, conv_w, conv_b, w_x, w_dt, b_dt, a_log, d_skip, w_out, conv_state, ssm_state):
        tokens, width = residual.shape
        inner = w_out.shape[1]
        state = a_log.shape[1]
        lane_tiles = inner // 128
        chunk = tokens // CHUNKS
        own = chunk // 8
        w_view = w_in.reshape(2, width, 2, lane_tiles, 128).transpose(0, 1, 3, 2, 4)
        conv_view = conv_state.transpose(0, 2, 1, 3)
        vmem = pl.BlockSpec(memory_space=pltpu.VMEM)
        anywhere = pl.BlockSpec(memory_space=pl.ANY)
        hbm = pl.BlockSpec(memory_space=pltpu.HBM)
        f32, bf16 = jnp.float32, jnp.bfloat16
        r_val, conv_val, s0, s1 = pl.pallas_call(
            mamba_kernel,
            name="mamba",
            out_shape=[
                pltpu.VMEM((tokens, width), f32),
                pltpu.VMEM((2, 3, tokens, inner), bf16),
                pltpu.VMEM((tokens, state, inner), f32),
                pltpu.VMEM((tokens, state, inner), f32),
            ],
            in_specs=[hbm] * 5 + [vmem] * 8,
            out_specs=[vmem] * 4,
            scratch_shapes=[
                pltpu.VMEM((tokens, width), f32),
                pltpu.VMEM((lane_tiles, width, 2, 128), bf16),
                pltpu.VMEM((2, width, 2 * inner), bf16),
                pltpu.VMEM((2, inner, width), bf16),
                pltpu.VMEM((2, tokens, inner), bf16),
                pltpu.VMEM((2, 128, inner), bf16),
                pltpu.VMEM((tokens, width), bf16),
                pltpu.VMEM((tokens, inner), bf16),
                pltpu.VMEM((tokens, inner), bf16),
                pltpu.VMEM((tokens, width), bf16),
                pltpu.VMEM((CHUNKS, 4 * own, width), bf16),
                pltpu.VMEM((CHUNKS, 2 * own, width), bf16),
                pltpu.VMEM((CHUNKS, own, width), bf16),
                pltpu.VMEM((CHUNKS, own, width), f32),
                pltpu.VMEM((tokens, 128), f32),
                pltpu.VMEM((3, tokens, 128), bf16),
                pltpu.VMEM((3, tokens, 128), bf16),
                pltpu.VMEM((chunk, inner), f32),
                pltpu.VMEM((chunk, inner), f32),
                pltpu.VMEM((lane_tiles, chunk * 8, 128), f32),
                pltpu.VMEM((chunk, inner), bf16),
                pltpu.SemaphoreType.DMA((COPIES + 1, 2, CHUNKS)),
                pltpu.SemaphoreType.DMA((COPIES + 1, 2, CHUNKS)),
                pltpu.SemaphoreType.DMA((20,)),
                pltpu.SemaphoreType.DMA((2, CHUNKS)),
            ],
            compiler_params=pltpu.CompilerParams(collective_id=0, has_side_effects=True, vmem_limit_bytes=30 * 2**20),
        )(residual, w_view, w_out, conv_view, ssm_state, norm_w, conv_w, conv_b, w_x, w_dt, b_dt, a_log, d_skip)
        r_new, conv_new, ssm_new = pl.pallas_call(
            dump_kernel,
            name="dump",
            out_shape=[
                jax.ShapeDtypeStruct((tokens, width), f32),
                jax.ShapeDtypeStruct((2, 3, tokens, inner), bf16),
                jax.ShapeDtypeStruct(ssm_state.shape, f32),
            ],
            in_specs=[anywhere] * 4,
            out_specs=[hbm] * 3,
            scratch_shapes=[pltpu.SemaphoreType.DMA((4,))],
            compiler_params=pltpu.CompilerParams(vmem_limit_bytes=2**20),
        )(r_val, conv_val, s0, s1)
        return r_new, conv_new.transpose(0, 2, 1, 3), ssm_new

    cache_spec = P(None, 'dp', None, 'tp')
    in_specs = (P('dp', None), P(None, None), P(None, None, None, 'tp'), P(None, None, 'tp'), P(None, 'tp'), P(None, 'tp', None), P(None, None, 'tp'), P(None, 'tp'), P(None, None, 'tp'), P(None, 'tp'), P(None, 'tp', None), cache_spec, cache_spec)
    out_specs = (P('dp', None), cache_spec, cache_spec)
    return jax.shard_map(device_step, mesh=mesh, in_specs=in_specs, out_specs=out_specs, check_vma=False)
```

time: 291 us -> 104 us (0.36)
  waiting for transfers between devices: 169 us -> 0 us
  Pallas kernels: 0 us -> 103 us
  other arithmetic: 78.5 us -> 0 us
  matrix products: 15.2 us -> 0 us
  between operations: 14.4 us -> 0.64 us
  local copies, waits for them, and re-layouts: 13.2 us -> 0 us
    psum x4 -> x0, waiting for transfers between devices: 169 us -> none  [the longest x2 87.7 us: device_step(): proj_sum = lax.psum(proj_part, 'tp').astype(jnp.float32)]
    pallas_call x0 -> x2, Pallas kernels: none -> 103 us  [the longest x1 93 us: device_step(): pl.pallas_call(mamba_kernel, name='mamba', out_shape=[pltpu.VMEM((tokens,...]
    add x3 -> x0, other arithmetic: 27.6 us -> none  [the longest x1 23.4 us: device_step(): decay_fac * ssm_state[layer_idx]]
    reduce_sum x10 -> x0, other arithmetic: 23.8 us -> none  [the longest x2 17.8 us: device_step(): jnp.sum(new_ssm * c_vec[:, :, None], axis=1) + d_skip[layer_idx] * x_float]
    another operation x4 -> x0, other arithmetic: 21.4 us -> none  [device_step(): return (residual, jnp.stack(conv_list), jnp.stack(ssm_list))]
    dot_general x8 -> x0, matrix products: 15.2 us -> none  [the longest x2 4.79 us: device_step(): jnp.dot(dt_low, w_dt[layer_idx], preferred_element_type=jnp.float32)]
    slice x5 -> x0, local copies, waits for them, and re-layouts: 7.1 us -> none  [the longest x1 4.27 us: device_step(): w_in[layer_idx]]
    unnamed x88 -> x0, local copies, waits for them, and re-layouts: 4.87 us -> none
  transfers between devices with their start and end apart: 4 -> 0, of which waited for: 4 -> 0; matrix products, arithmetic and copies ran while one was open for 9% -> 0% of each run, Pallas kernels for 0% -> 0%
where the time goes in v1:
time: 104 us
  Pallas kernels  103 us (99%)
    pallas_call x1, Pallas kernels, device_step(): pl.pallas_call(mamba_kernel, name='mamba', out_shape=[pltpu.VMEM((tokens,...  93 us
    pallas_call x1, Pallas kernels, device_step(): pl.pallas_call(dump_kernel, name='dump', out_shape=[jax.ShapeDtypeStruct(...  10.3 us

profile of v1, /device:TPU:0, one launch (start us, length us, event | category | flops | bytes accessed | tf_op | source)
XLA Modules:
  0.0 104.0 jit_solution(15200678875650889524)
XLA Ops:
  0.6 93.0 %mamba.1 = (f32[512,1536]{1,0:T(8,128)S(1)}, bf16[2,3,512,384]{3,2,1,0:T(8,128)(2,1)S(1)}, f32[512,16,384]{2,1,0:T(8,128)S(1)}, f32[512,16,384]{2,1,0:T(8,128)S(1)}) custom-call(f32[512,1536]{1,0:T(8,128)} %residual.1, bf16[2,1536,3,2,128]{4,3,2,1,0:T(2,128)(2,1)} %bitcast.5, bf16[2,384,1536]{2,1,0:T(8,128)(2,1)} %w_out.1, bf16[2,3,512,384]{3,2,1,0:T(8,128)(2,1)} %bitcast.6, ...), custom_call_target="tpu_custom_call" | custom-call | tf_op jit(solution)/shard_map/mamba/pallas_call | solution.py:355
  93.7 10.3 %dump.1 = (f32[512,1536]{1,0:T(8,128)}, bf16[2,3,512,384]{3,2,1,0:T(8,128)(2,1)}, f32[2,512,16,384]{3,2,1,0:T(8,128)}) custom-call(f32[512,1536]{1,0:T(8,128)S(1)} %get-tuple-element.10.r_val, bf16[2,3,512,384]{3,2,1,0:T(8,128)(2,1)S(1)} %get-tuple-element.11.conv_val, f32[512,16,384]{2,1,0:T(8,128)S(1)} %get-tuple-element.12.ssm0, ...), custom_call_target="tpu_custom_call" | custom-call | tf_op jit(solution)/shard_map/dump/pallas_call | solution.py:395

commit v2 on v1

v2 whole, which is shorter than its diff:
```python
import functools

import jax
import jax.numpy as jnp
from jax import lax
from jax.experimental import pallas as pl
from jax.experimental.pallas import tpu as pltpu
from jax.sharding import PartitionSpec as P

MESH = pl.DeviceIdType.MESH
LOG2E = 1.4426950408889634
CHUNKS = 4
KINDS = 8
ORDER = (0, 3, 2, 0, 1, 4, 4, 4, 4, 1, 2, 3, 0, 1, 0, 2, 1, 2, 3, 0, 3, 1, 2, 0, 0, 3, 0, 1, 1, 2, 1, 2, 3, 2, 3, 0, 3, 1, 0, 2, 1, 2, 3, 0, 3, 2, 1, 0, 3, 2, 1, 3, 1, 0, 2, 3)

GROUP = 16
ORDER_FIRST = tuple(dict.fromkeys(q for q in ORDER if q < CHUNKS))


def rms_scale(vector, epsilon):
    return lax.rsqrt(jnp.mean(vector * vector, axis=-1, keepdims=True) + epsilon)


def mamba_kernel(
    residual, w_in, w_out, conv_state, ssm_state, norm_w_hbm, conv_w_hbm, conv_b_hbm, w_x_hbm, w_dt_hbm, b_dt_hbm, a_log_hbm, d_skip_hbm,
    r_out, conv_out, ssm0, ssm1,
    res, w_raw, w_xz, wo, conv_old, norm_w, conv_w, conv_b, w_x, w_dt, b_dt, a_log, d_skip, hid, xc_buf, z_buf, part, half_in, half_in2, o_acc,
    p_acc, p_send, p_recv, dt_buf, dx_buf, y_part, yg_buf, send_sem, recv_sem, load_sem, small_sem, state_sem,
):
    layers = 2
    tokens, width = res.shape
    chunk = tokens // CHUNKS
    half = chunk // 2
    inner = wo.shape[1]
    rank = w_dt_hbm.shape[1]
    state = a_log.shape[1]
    lane_tiles = inner // 128
    ssm_bufs = (ssm0, ssm1)

    tp = lax.axis_index("tp")
    core = lax.rem(tp, 2)
    pos_x = lax.rem(lax.div(tp, 2), 2)
    pos_y = lax.div(tp, 4)
    bit_a = pos_x * (1 - core) + pos_y * core
    bit_b = pos_y * (1 - core) + pos_x * core
    peer_c = tp + 1 - 2 * core
    peer_a = tp + (1 - 2 * bit_a) * (2 + 2 * core)
    peer_b = tp + (1 - 2 * bit_b) * (4 - 2 * core)
    peer_d = tp + (1 - 2 * pos_x) * 2 + (1 - 2 * pos_y) * 4
    peers = (peer_c, peer_a, peer_b, peer_d)

    barrier = pltpu.get_barrier_semaphore()
    for peer in peers:
        pl.semaphore_signal(barrier, inc=1, device_id={"tp": peer}, device_id_type=MESH)

    def rows_of(q):
        return pl.ds(q * chunk, chunk)

    def half_rows(q, which):
        return pl.ds(pl.multiple_of(q * chunk + which * half, half), half)

    def remote(kind, layer, q, src, dst, peer):
        return pltpu.make_async_remote_copy(
            src_ref=src, dst_ref=dst, send_sem=send_sem.at[kind, layer, q], recv_sem=recv_sem.at[kind, layer, q],
            device_id={"tp": peer}, device_id_type=MESH,
        )

    def p_copy(step, layer, q):
        src = p_send.at[min(step, 1), rows_of(q)]
        return remote(step, layer, q, src, p_recv.at[step, rows_of(q)], peers[step])

    def o_copy(step, layer, q):
        if step == 0:
            return remote(4, layer, q, part.at[half_rows(q, 1 - core)], half_in.at[0, q], peer_c)
        return remote(4 + step, layer, q, half_in2.at[step - 1, q], half_in.at[step, q], peers[step])

    def h_copy(layer, q):
        ref = hid.at[half_rows(q, core)]
        return remote(7, layer, q, ref, ref, peer_c)

    def w_load(layer, tile):
        return pltpu.make_async_copy(w_in.at[layer, :, tile], w_raw.at[layer, tile], load_sem.at[layer * lane_tiles + tile])

    def res_load(q):
        return pltpu.make_async_copy(residual.at[rows_of(q)], res.at[rows_of(q)], load_sem.at[6 + q])

    def wo_load(layer):
        return pltpu.make_async_copy(w_out.at[layer], wo.at[layer], load_sem.at[10 + layer])

    def conv_load(layer, row):
        dst = conv_old.at[layer] if row == 0 else conv_out.at[layer, row - 1]
        return pltpu.make_async_copy(conv_state.at[layer, row], dst, load_sem.at[12 + 3 * layer + row])

    def state_load(layer, q):
        return pltpu.make_async_copy(ssm_state.at[layer, rows_of(q)], ssm_bufs[layer].at[rows_of(q)], state_sem.at[layer, q])

    small = [
        pltpu.make_async_copy(norm_w_hbm, norm_w, small_sem.at[0]),
        pltpu.make_async_copy(conv_w_hbm, conv_w, small_sem.at[1]),
        pltpu.make_async_copy(conv_b_hbm, conv_b, small_sem.at[2]),
        pltpu.make_async_copy(w_x_hbm, w_x, small_sem.at[3]),
        pltpu.make_async_copy(w_dt_hbm, w_dt.at[:, pl.ds(0, rank)], small_sem.at[4]),
        pltpu.make_async_copy(b_dt_hbm, b_dt, small_sem.at[5]),
        pltpu.make_async_copy(a_log_hbm, a_log, small_sem.at[6]),
        pltpu.make_async_copy(d_skip_hbm, d_skip, small_sem.at[7]),
    ]
    small[0].start()
    res_load(ORDER[0]).start()
    for tile in range(lane_tiles):
        w_load(0, tile).start()
    for q in range(CHUNKS):
        if q != ORDER[0]:
            res_load(q).start()
    for row in range(3):
        conv_load(0, row).start()
    for copy in small[1:]:
        copy.start()
    for layer in range(layers):
        w_dt[layer, rank:] = jnp.zeros((128 - rank, inner), jnp.bfloat16)

    def split_weights(layer, first, count):
        row = lax.broadcasted_iota(jnp.int32, (256, 256), 0)
        col = lax.broadcasted_iota(jnp.int32, (256, 256), 1)
        want = jnp.where(row < 128, 2 * row, 2 * row - 255)
        pick = jnp.where(col == want, 1.0, 0.0).astype(jnp.bfloat16)
        for i in range(count):
            src = pl.ds(pl.multiple_of((first + i) * 256, 256), 256)
            raw = [w_raw.at[layer, tile].reshape(2 * width, 128)[src, :] for tile in range(lane_tiles)]
            both = jnp.dot(pick, jnp.concatenate(raw, axis=1), preferred_element_type=jnp.float32).astype(jnp.bfloat16)
            dst = pl.ds(pl.multiple_of((first + i) * 128, 128), 128)
            w_xz[layer, dst, :inner] = both[:128]
            w_xz[layer, dst, inner:] = both[128:]

    blocks = width // 128
    split_step = 3

    def first_norm(q):
        res_load(q).wait()

        @pl.loop(0, chunk // 32)
        def _(i):
            sub = pl.ds(pl.multiple_of(q * chunk + i * 32, 32), 32)
            r = res[sub, :]
            hid[sub, :] = (r * rms_scale(r, 1e-5) * norm_w[0:1, :].astype(jnp.float32)).astype(jnp.bfloat16)

    small[0].wait()
    first_norm(ORDER[0])
    for tile in range(lane_tiles):
        w_load(0, tile).wait()

    @pl.loop(0, blocks // split_step)
    def _(step):
        split_weights(0, step * split_step, split_step)

    for tile in range(lane_tiles):
        w_load(1, tile).start()
    for q in ORDER_FIRST:
        state_load(0, q).start()
    wo_load(0).start()
    for row in range(3):
        conv_load(0, row).wait()
    for copy in small[1:]:
        copy.wait()
    pl.semaphore_wait(barrier, 4)

    def stage_in(layer, q):
        rows = rows_of(q)
        if layer == 0:
            if q != ORDER[0]:
                first_norm(q)
        else:
            h_copy(layer - 1, q).wait()
        xz = jnp.dot(hid[rows, :], w_xz[layer], preferred_element_type=jnp.float32)
        x_val = xz[:, :inner].astype(jnp.bfloat16)
        z_buf[rows, :] = xz[:, inner:].astype(jnp.bfloat16)
        conv_out[layer, 2, rows, :] = x_val
        taps = conv_w[layer].astype(jnp.float32)
        pre = conv_old[layer, rows, :].astype(jnp.float32) * taps[0:1]
        pre = pre + conv_out[layer, 0, rows, :].astype(jnp.float32) * taps[1:2]
        pre = pre + conv_out[layer, 1, rows, :].astype(jnp.float32) * taps[2:3]
        pre = pre + x_val.astype(jnp.float32) * taps[3:4]
        pre = pre + conv_b[layer:layer + 1, :].astype(jnp.float32)
        xc = (pre * jax.nn.sigmoid(pre)).astype(jnp.bfloat16)
        xc_buf[rows, :] = xc
        p = jnp.dot(xc, w_x[layer], preferred_element_type=jnp.float32)
        p_acc[rows, :] = p
        p_send[0, rows, :] = p.astype(jnp.bfloat16)
        p_copy(0, layer, q).start()

    def stage_p(layer, q):
        rows = rows_of(q)
        p_copy(0, layer, q).wait()
        p = p_acc[rows, :] + p_recv[0, rows, :].astype(jnp.float32)
        p_acc[rows, :] = p
        p_send[1, rows, :] = p.astype(jnp.bfloat16)
        for step in (3, 1, 2):
            p_copy(step, layer, q).start()

    def stage_ssm(layer, q):
        rows = rows_of(q)
        state_buf = ssm_bufs[layer]
        p = p_acc[rows, :]
        for step in (1, 2, 3):
            p_copy(step, layer, q).wait()
            p = p + p_recv[step, rows, :].astype(jnp.float32)
        lane = lax.broadcasted_iota(jnp.int32, p.shape, 1)
        square = p * p
        is_dt = lane < rank
        is_b = jnp.logical_and(lane >= rank, lane < rank + state)

        def scale_of(mask, count):
            total = jnp.sum(jnp.where(mask, square, 0.0), axis=1, keepdims=True)
            return lax.rsqrt(total * (1.0 / count) + 1e-6)

        scale_dt = scale_of(is_dt, rank)
        scale_b = scale_of(is_b, state)
        scale_c = scale_of(lane >= rank + state, state)
        normed = p * jnp.where(is_dt, scale_dt, jnp.where(is_b, scale_b, scale_c))
        dt_low = jnp.where(is_dt, normed, 0.0).astype(jnp.bfloat16)
        pre = jnp.dot(dt_low, w_dt[layer], preferred_element_type=jnp.float32) + b_dt[layer:layer + 1, :]
        dt = jnp.maximum(pre, 0.0) + jnp.log1p(jnp.exp(-jnp.abs(pre)))
        dt_buf[...] = dt
        dx_buf[...] = dt * xc_buf[rows, :].astype(jnp.float32)
        turned = normed.T
        b_cols = turned[rank:rank + state, :]
        c_cols = turned[rank + state:, :]
        decay_rate = jnp.exp(a_log[layer]) * (-LOG2E)
        state_load(layer, q).wait()

        def scan_group(g, carry):
            b_now, c_now = carry
            for j in range(GROUP):
                token = g * GROUP + j
                dt_row = dt_buf[pl.ds(token, 1), :]
                dx_row = dx_buf[pl.ds(token, 1), :]
                old = state_buf[q * chunk + token]
                new = jnp.exp2(dt_row * decay_rate) * old + dx_row * b_now[:, j:j + 1]
                state_buf[q * chunk + token] = new
                weighted = new * c_now[:, j:j + 1]
                partial = weighted[:8] + weighted[8:]
                for tile in range(lane_tiles):
                    y_part[tile, pl.ds(pl.multiple_of(token * 8, 8), 8), :] = partial[:, tile * 128:(tile + 1) * 128]
            return pltpu.roll(b_now, chunk - GROUP, 1), pltpu.roll(c_now, chunk - GROUP, 1)

        lax.fori_loop(0, chunk // GROUP, scan_group, (b_cols, c_cols))

        @pl.loop(0, chunk // 32)
        def _(g):
            for k in range(4):
                first = g * 256 + k * 64
                by_tile = []
                for tile in range(lane_tiles):
                    terms = [y_part[tile, pl.ds(first + sub, 8, stride=8), :] for sub in range(8)]
                    while len(terms) > 1:
                        terms = [terms[i] + terms[i + 1] for i in range(0, len(terms), 2)]
                    by_tile.append(terms[0])
                y_buf_rows = pl.ds(pl.multiple_of(g * 32 + k * 8, 8), 8)
                dt_buf[y_buf_rows, :] = jnp.concatenate(by_tile, axis=1)
            sub = pl.ds(pl.multiple_of(g * 32, 32), 32)
            sub_rows = pl.ds(pl.multiple_of(q * chunk + g * 32, 32), 32)
            y = dt_buf[sub, :] + d_skip[layer:layer + 1, :] * xc_buf[sub_rows, :].astype(jnp.float32)
            z = z_buf[sub_rows, :].astype(jnp.float32)
            yg_buf[sub, :] = (y * (z * jax.nn.sigmoid(z))).astype(jnp.bfloat16)

        if q == ORDER_FIRST[0]:
            wo_load(layer).wait()
        part[rows, :] = jnp.dot(yg_buf[...], wo[layer], preferred_element_type=jnp.float32).astype(jnp.bfloat16)
        o_copy(0, layer, q).start()

    def stage_o(step, layer, q):
        o_copy(step - 1, layer, q).wait()
        mine = part[half_rows(q, core), :] if step == 1 else half_in2[0, q]
        half_in2[step - 1, q] = (mine.astype(jnp.float32) + half_in[step - 1, q].astype(jnp.float32)).astype(jnp.bfloat16)
        o_copy(step, layer, q).start()

    def stage_own(layer, q):
        o_copy(2, layer, q).wait()
        mine = half_rows(q, core)

        @pl.loop(0, half // 16)
        def _(i):
            sub = pl.ds(pl.multiple_of(i * 16, 16), 16)
            dst = pl.ds(pl.multiple_of(q * chunk + core * half + i * 16, 16), 16)
            o_val = half_in2[1, q, sub, :].astype(jnp.float32) + half_in[2, q, sub, :].astype(jnp.float32)
            if layer == 0:
                o_acc[q, sub, :] = o_val
                r = res[dst, :] + o_val
                hid[dst, :] = (r * rms_scale(r, 1e-5) * norm_w[1:2, :].astype(jnp.float32)).astype(jnp.bfloat16)
            else:
                hid[dst, :] = (o_acc[q, sub, :] + o_val).astype(jnp.bfloat16)

        h_copy(layer, q).start()

    def stage_out(q):
        h_copy(layers - 1, q).wait()
        rows = rows_of(q)
        r_out[rows, :] = res[rows, :] + hid[rows, :].astype(jnp.float32)

    stages = []
    for layer in range(layers):
        stages.append(functools.partial(stage_in, layer))
        stages.append(functools.partial(stage_p, layer))
        stages.append(functools.partial(stage_ssm, layer))
        stages.append(functools.partial(stage_o, 1, layer))
        stages.append(functools.partial(stage_o, 2, layer))
        stages.append(functools.partial(stage_own, layer))
    stages.append(stage_out)

    progress = [0] * CHUNKS
    fills = 0
    for q in ORDER:
        if q == CHUNKS:
            if fills == 0:
                for tile in range(lane_tiles):
                    w_load(1, tile).wait()
                for row in range(3):
                    conv_load(1, row).start()
                wo_load(1).start()
                for chunk_index in ORDER_FIRST:
                    state_load(1, chunk_index).start()
            split_weights(1, fills * split_step, split_step)
            fills += 1
        else:
            if q == ORDER_FIRST[0] and progress[q] == 6:
                for row in range(3):
                    conv_load(1, row).wait()
            stages[progress[q]](q)
            progress[q] += 1


def dump_kernel(r_val, conv_val, ssm0, ssm1, r_hbm, conv_hbm, ssm_hbm, sems):
    copies = [
        pltpu.make_async_copy(ssm0, ssm_hbm.at[0], sems.at[0]),
        pltpu.make_async_copy(ssm1, ssm_hbm.at[1], sems.at[1]),
        pltpu.make_async_copy(conv_val, conv_hbm, sems.at[2]),
        pltpu.make_async_copy(r_val, r_hbm, sems.at[3]),
    ]
    for copy in copies:
        copy.start()
    for copy in copies:
        copy.wait()


def solution(mesh):
    def device_step(residual, norm_w, w_in, conv_w, conv_b, w_x, w_dt, b_dt, a_log, d_skip, w_out, conv_state, ssm_state):
        tokens, width = residual.shape
        inner = w_out.shape[1]
        state = a_log.shape[1]
        lane_tiles = inner // 128
        chunk = tokens // CHUNKS
        half = chunk // 2
        w_view = w_in.reshape(2, width, 2, lane_tiles, 128).transpose(0, 1, 3, 2, 4)
        conv_view = conv_state.transpose(0, 2, 1, 3)
        vmem = pl.BlockSpec(memory_space=pltpu.VMEM)
        anywhere = pl.BlockSpec(memory_space=pl.ANY)
        hbm = pl.BlockSpec(memory_space=pltpu.HBM)
        f32, bf16 = jnp.float32, jnp.bfloat16
        r_val, conv_val, s0, s1 = pl.pallas_call(
            mamba_kernel,
            name="mamba",
            out_shape=[
                pltpu.VMEM((tokens, width), f32),
                pltpu.VMEM((2, 3, tokens, inner), bf16),
                pltpu.VMEM((tokens, state, inner), f32),
                pltpu.VMEM((tokens, state, inner), f32),
            ],
            in_specs=[hbm] * 13,
            out_specs=[vmem] * 4,
            scratch_shapes=[
                pltpu.VMEM((tokens, width), f32),
                pltpu.VMEM((2, lane_tiles, width, 2, 128), bf16),
                pltpu.VMEM((2, width, 2 * inner), bf16),
                pltpu.VMEM((2, inner, width), bf16),
                pltpu.VMEM((2, tokens, inner), bf16),
                pltpu.VMEM(norm_w.shape, bf16),
                pltpu.VMEM(conv_w.shape, bf16),
                pltpu.VMEM(conv_b.shape, bf16),
                pltpu.VMEM(w_x.shape, bf16),
                pltpu.VMEM((2, 128, inner), bf16),
                pltpu.VMEM(b_dt.shape, f32),
                pltpu.VMEM(a_log.shape, f32),
                pltpu.VMEM(d_skip.shape, f32),
                pltpu.VMEM((tokens, width), bf16),
                pltpu.VMEM((tokens, inner), bf16),
                pltpu.VMEM((tokens, inner), bf16),
                pltpu.VMEM((tokens, width), bf16),
                pltpu.VMEM((3, CHUNKS, half, width), bf16),
                pltpu.VMEM((2, CHUNKS, half, width), bf16),
                pltpu.VMEM((CHUNKS, half, width), f32),
                pltpu.VMEM((tokens, 128), f32),
                pltpu.VMEM((2, tokens, 128), bf16),
                pltpu.VMEM((4, tokens, 128), bf16),
                pltpu.VMEM((chunk, inner), f32),
                pltpu.VMEM((chunk, inner), f32),
                pltpu.VMEM((lane_tiles, chunk * 8, 128), f32),
                pltpu.VMEM((chunk, inner), bf16),
                pltpu.SemaphoreType.DMA((KINDS, 2, CHUNKS)),
                pltpu.SemaphoreType.DMA((KINDS, 2, CHUNKS)),
                pltpu.SemaphoreType.DMA((18,)),
                pltpu.SemaphoreType.DMA((8,)),
                pltpu.SemaphoreType.DMA((2, CHUNKS)),
            ],
            compiler_params=pltpu.CompilerParams(collective_id=0, has_side_effects=True, vmem_limit_bytes=32 * 2**20),
        )(residual, w_view, w_out, conv_view, ssm_state, norm_w, conv_w, conv_b, w_x, w_dt, b_dt, a_log, d_skip)
        r_new, conv_new, ssm_new = pl.pallas_call(
            dump_kernel,
            name="dump",
            out_shape=[
                jax.ShapeDtypeStruct((tokens, width), f32),
                jax.ShapeDtypeStruct((2, 3, tokens, inner), bf16),
                jax.ShapeDtypeStruct(ssm_state.shape, f32),
            ],
            in_specs=[anywhere] * 4,
            out_specs=[hbm] * 3,
            scratch_shapes=[pltpu.SemaphoreType.DMA((4,))],
            compiler_params=pltpu.CompilerParams(vmem_limit_bytes=2**20),
        )(r_val, conv_val, s0, s1)
        return r_new, conv_new.transpose(0, 2, 1, 3), ssm_new

    cache_spec = P(None, 'dp', None, 'tp')
    in_specs = (P('dp', None), P(None, None), P(None, None, None, 'tp'), P(None, None, 'tp'), P(None, 'tp'), P(None, 'tp', None), P(None, None, 'tp'), P(None, 'tp'), P(None, None, 'tp'), P(None, 'tp'), P(None, 'tp', None), cache_spec, cache_spec)
    out_specs = (P('dp', None), cache_spec, cache_spec)
    return jax.shard_map(device_step, mesh=mesh, in_specs=in_specs, out_specs=out_specs, check_vma=False)
```

time: 104 us -> 78.9 us (0.76)
  Pallas kernels: 103 us -> 78.1 us
    pallas_call x1, Pallas kernels: 93 us -> 67.7 us  [device_step(): pl.pallas_call(mamba_kernel, name='mamba', out_shape=[pltpu.VMEM((tokens,...]
where the time goes in v2:
time: 78.9 us; the launch traced here: 78.7 us
  Pallas kernels  78.1 us (99%)
    pallas_call x1, Pallas kernels, device_step(): pl.pallas_call(mamba_kernel, name='mamba', out_shape=[pltpu.VMEM((tokens,...  67.7 us
    pallas_call x1, Pallas kernels, device_step(): pl.pallas_call(dump_kernel, name='dump', out_shape=[jax.ShapeDtypeStruct(...  10.3 us

profile of v2, /device:TPU:0, one launch (start us, length us, event | category | flops | bytes accessed | tf_op | source)
XLA Modules:
  0.0 78.7 jit_solution(5000636686786757652)
XLA Ops:
  0.6 67.7 %mamba.1 = (f32[512,1536]{1,0:T(8,128)S(1)}, bf16[2,3,512,384]{3,2,1,0:T(8,128)(2,1)S(1)}, f32[512,16,384]{2,1,0:T(8,128)S(1)}, f32[512,16,384]{2,1,0:T(8,128)S(1)}) custom-call(f32[512,1536]{1,0:T(8,128)} %residual.1, bf16[2,1536,3,2,128]{4,3,2,1,0:T(2,128)(2,1)} %bitcast.5, bf16[2,384,1536]{2,1,0:T(8,128)(2,1)} %w_out.1, bf16[2,3,512,384]{3,2,1,0:T(8,128)(2,1)} %bitcast.6, ...), custom_call_target="tpu_custom_call" | custom-call | tf_op jit(solution)/shard_map/mamba/pallas_call | solution.py:358
  68.4 10.3 %dump.1 = (f32[512,1536]{1,0:T(8,128)}, bf16[2,3,512,384]{3,2,1,0:T(8,128)(2,1)}, f32[2,512,16,384]{3,2,1,0:T(8,128)}) custom-call(f32[512,1536]{1,0:T(8,128)S(1)} %get-tuple-element.10.r_val, bf16[2,3,512,384]{3,2,1,0:T(8,128)(2,1)S(1)} %get-tuple-element.11.conv_val, f32[512,16,384]{2,1,0:T(8,128)S(1)} %get-tuple-element.12.ssm0, ...), custom_call_target="tpu_custom_call" | custom-call | tf_op jit(solution)/shard_map/dump/pallas_call | solution.py:405

commit v3 on v2

--- a/solution.py
+++ b/solution.py
@@ -3,6 +3,7 @@
 import jax
 import jax.numpy as jnp
 from jax import lax
+from jax.experimental.layout import Layout, with_layout_constraint
 from jax.experimental import pallas as pl
 from jax.experimental.pallas import tpu as pltpu
 from jax.sharding import PartitionSpec as P
@@ -10,10 +11,11 @@
 MESH = pl.DeviceIdType.MESH
 LOG2E = 1.4426950408889634
 CHUNKS = 4
-KINDS = 8
-ORDER = (0, 3, 2, 0, 1, 4, 4, 4, 4, 1, 2, 3, 0, 1, 0, 2, 1, 2, 3, 0, 3, 1, 2, 0, 0, 3, 0, 1, 1, 2, 1, 2, 3, 2, 3, 0, 3, 1, 0, 2, 1, 2, 3, 0, 3, 2, 1, 0, 3, 2, 1, 3, 1, 0, 2, 3)
-
-GROUP = 16
+KINDS = 10
+ORDER = (0, 2, 1, 0, 1, 3, 4, 4, 2, 4, 3, 0, 1, 2, 0, 1, 3, 2, 3, 0, 1, 2, 3, 0, 1, 2, 0, 3, 1, 0, 1, 2, 0, 3, 1, 2, 3, 2, 3, 0, 1, 2, 0, 1, 3, 2, 3, 0, 1, 2, 3, 0, 1, 2, 3, 0, 1, 2, 1, 3, 0, 2, 3)
+
+GROUP = 64
+DUMP_PIECES = 4
 ORDER_FIRST = tuple(dict.fromkeys(q for q in ORDER if q < CHUNKS))
 
 
@@ -24,13 +26,14 @@
 def mamba_kernel(
     residual, w_in, w_out, conv_state, ssm_state, norm_w_hbm, conv_w_hbm, conv_b_hbm, w_x_hbm, w_dt_hbm, b_dt_hbm, a_log_hbm, d_skip_hbm,
     r_out, conv_out, ssm0, ssm1,
-    res, w_raw, w_xz, wo, conv_old, norm_w, conv_w, conv_b, w_x, w_dt, b_dt, a_log, d_skip, hid, xc_buf, z_buf, part, half_in, half_in2, o_acc,
-    p_acc, p_send, p_recv, dt_buf, dx_buf, y_part, yg_buf, send_sem, recv_sem, load_sem, small_sem, state_sem,
+    res, w_raw, w_xz, wo, conv_old, norm_w, conv_w, conv_b, w_x, w_dt, b_dt, a_log, d_skip, hid, xc_buf, z_buf, part, half_in, quart_in, quart_sum, pair_in, o_acc,
+    p_acc, p_send, p_recv, rate_buf, dt_buf, dx_buf, y_part, yg_buf, send_sem, recv_sem, load_sem, small_sem, state_sem,
 ):
     layers = 2
     tokens, width = res.shape
     chunk = tokens // CHUNKS
     half = chunk // 2
+    quart = chunk // 4
     inner = wo.shape[1]
     rank = w_dt_hbm.shape[1]
     state = a_log.shape[1]
@@ -59,6 +62,9 @@
     def half_rows(q, which):
         return pl.ds(pl.multiple_of(q * chunk + which * half, half), half)
 
+    def quart_rows(q, which_half, which):
+        return pl.ds(pl.multiple_of(q * chunk + which_half * half + which * quart, quart), quart)
+
     def remote(kind, layer, q, src, dst, peer):
         return pltpu.make_async_remote_copy(
             src_ref=src, dst_ref=dst, send_sem=send_sem.at[kind, layer, q], recv_sem=recv_sem.at[kind, layer, q],
@@ -71,18 +77,20 @@
 
     def o_copy(step, layer, q):
         if step == 0:
-            return remote(4, layer, q, part.at[half_rows(q, 1 - core)], half_in.at[0, q], peer_c)
-        return remote(4 + step, layer, q, half_in2.at[step - 1, q], half_in.at[step, q], peers[step])
-
-    def h_copy(layer, q):
-        ref = hid.at[half_rows(q, core)]
-        return remote(7, layer, q, ref, ref, peer_c)
-
-    def w_load(layer, tile):
-        return pltpu.make_async_copy(w_in.at[layer, :, tile], w_raw.at[layer, tile], load_sem.at[layer * lane_tiles + tile])
+            return remote(4, layer, q, part.at[half_rows(q, 1 - core)], half_in.at[q], peer_c)
+        if step == 1:
+            return remote(5, layer, q, part.at[quart_rows(q, core, 1 - bit_a)], quart_in.at[q], peer_a)
+        return remote(6, layer, q, quart_sum.at[q], pair_in.at[q], peer_b)
+
+    def h_copy(step, layer, q):
+        ref = hid.at[quart_rows(q, core, 1 - bit_a if step == 2 else bit_a)]
+        return remote(7 + step, layer, q, ref, ref, peer_a if step == 0 else peer_c)
+
+    def w_load(layer):
+        return pltpu.make_async_copy(w_in.at[layer], w_raw.at[layer], load_sem.at[layer])
 
     def res_load(q):
-        return pltpu.make_async_copy(residual.at[rows_of(q)], res.at[rows_of(q)], load_sem.at[6 + q])
+        return pltpu.make_async_copy(residual.at[rows_of(q)], res.at[rows_of(q)], load_sem.at[18 + q])
 
     def wo_load(layer):
         return pltpu.make_async_copy(w_out.at[layer], wo.at[layer], load_sem.at[10 + layer])
@@ -106,8 +114,7 @@
     ]
     small[0].start()
     res_load(ORDER[0]).start()
-    for tile in range(lane_tiles):
-        w_load(0, tile).start()
+    w_load(0).start()
     for q in range(CHUNKS):
         if q != ORDER[0]:
             res_load(q).start()
@@ -118,21 +125,29 @@
     for layer in range(layers):
         w_dt[layer, rank:] = jnp.zeros((128 - rank, inner), jnp.bfloat16)
 
+    span = 32
+    packed = span * lane_tiles * 2
+    blocks = width // (2 * span)
+
     def split_weights(layer, first, count):
-        row = lax.broadcasted_iota(jnp.int32, (256, 256), 0)
-        col = lax.broadcasted_iota(jnp.int32, (256, 256), 1)
-        want = jnp.where(row < 128, 2 * row, 2 * row - 255)
+        row = lax.broadcasted_iota(jnp.int32, (packed, packed), 0)
+        col = lax.broadcasted_iota(jnp.int32, (packed, packed), 1)
+        group = lax.div(row, span)
+        want = lax.rem(row, span) * (2 * lane_tiles) + lax.rem(group, lane_tiles) * 2 + lax.div(group, lane_tiles)
         pick = jnp.where(col == want, 1.0, 0.0).astype(jnp.bfloat16)
-        for i in range(count):
-            src = pl.ds(pl.multiple_of((first + i) * 256, 256), 256)
-            raw = [w_raw.at[layer, tile].reshape(2 * width, 128)[src, :] for tile in range(lane_tiles)]
-            both = jnp.dot(pick, jnp.concatenate(raw, axis=1), preferred_element_type=jnp.float32).astype(jnp.bfloat16)
-            dst = pl.ds(pl.multiple_of((first + i) * 128, 128), 128)
-            w_xz[layer, dst, :inner] = both[:128]
-            w_xz[layer, dst, inner:] = both[128:]
-
-    blocks = width // 128
-    split_step = 3
+
+        @pl.loop(0, count // 4)
+        def _(step):
+            for i in range(4):
+                block = first + step * 4 + i
+                raw = [w_raw[layer, pl.ds(pl.multiple_of((2 * block + k) * packed, packed), packed), :] for k in range(2)]
+                both = jnp.dot(pick, jnp.concatenate(raw, axis=1), preferred_element_type=jnp.float32).astype(jnp.bfloat16)
+                for k in range(2):
+                    dst = pl.ds(pl.multiple_of((2 * block + k) * span, span), span)
+                    for tile in range(2 * lane_tiles):
+                        w_xz[layer, dst, tile * 128:(tile + 1) * 128] = both[tile * span:(tile + 1) * span, k * 128:(k + 1) * 128]
+
+    split_step = 8
 
     def first_norm(q):
         res_load(q).wait()
@@ -145,15 +160,11 @@
 
     small[0].wait()
     first_norm(ORDER[0])
-    for tile in range(lane_tiles):
-        w_load(0, tile).wait()
-
-    @pl.loop(0, blocks // split_step)
-    def _(step):
-        split_weights(0, step * split_step, split_step)
-
-    for tile in range(lane_tiles):
-        w_load(1, tile).start()
+    w_load(0).wait()
+
+    split_weights(0, 0, blocks)
+
+    w_load(1).start()
     for q in ORDER_FIRST:
         state_load(0, q).start()
     wo_load(0).start()
@@ -163,13 +174,16 @@
         copy.wait()
     pl.semaphore_wait(barrier, 4)
 
+    wo_ready = [False] * layers
+
     def stage_in(layer, q):
         rows = rows_of(q)
         if layer == 0:
             if q != ORDER[0]:
                 first_norm(q)
         else:
-            h_copy(layer - 1, q).wait()
+            h_copy(1, layer - 1, q).wait()
+            h_copy(2, layer - 1, q).wait()
         xz = jnp.dot(hid[rows, :], w_xz[layer], preferred_element_type=jnp.float32)
         x_val = xz[:, :inner].astype(jnp.bfloat16)
         z_buf[rows, :] = xz[:, inner:].astype(jnp.bfloat16)
@@ -221,10 +235,10 @@
         dt = jnp.maximum(pre, 0.0) + jnp.log1p(jnp.exp(-jnp.abs(pre)))
         dt_buf[...] = dt
         dx_buf[...] = dt * xc_buf[rows, :].astype(jnp.float32)
-        turned = normed.T
+        turned = jnp.concatenate([normed] * (128 // chunk), axis=0).T
         b_cols = turned[rank:rank + state, :]
         c_cols = turned[rank + state:, :]
-        decay_rate = jnp.exp(a_log[layer]) * (-LOG2E)
+        rate_buf[...] = jnp.exp(a_log[layer]) * (-LOG2E)
         state_load(layer, q).wait()
 
         def scan_group(g, carry):
@@ -234,13 +248,13 @@
                 dt_row = dt_buf[pl.ds(token, 1), :]
                 dx_row = dx_buf[pl.ds(token, 1), :]
                 old = state_buf[q * chunk + token]
-                new = jnp.exp2(dt_row * decay_rate) * old + dx_row * b_now[:, j:j + 1]
+                new = jnp.exp2(dt_row * rate_buf[...]) * old + dx_row * b_now[:, j:j + 1]
                 state_buf[q * chunk + token] = new
                 weighted = new * c_now[:, j:j + 1]
                 partial = weighted[:8] + weighted[8:]
                 for tile in range(lane_tiles):
                     y_part[tile, pl.ds(pl.multiple_of(token * 8, 8), 8), :] = partial[:, tile * 128:(tile + 1) * 128]
-            return pltpu.roll(b_now, chunk - GROUP, 1), pltpu.roll(c_now, chunk - GROUP, 1)
+            return pltpu.roll(b_now, 128 - GROUP, 1), pltpu.roll(c_now, 128 - GROUP, 1)
 
         lax.fori_loop(0, chunk // GROUP, scan_group, (b_cols, c_cols))
 
@@ -262,37 +276,46 @@
             z = z_buf[sub_rows, :].astype(jnp.float32)
             yg_buf[sub, :] = (y * (z * jax.nn.sigmoid(z))).astype(jnp.bfloat16)
 
-        if q == ORDER_FIRST[0]:
+        if not wo_ready[layer]:
             wo_load(layer).wait()
+            wo_ready[layer] = True
         part[rows, :] = jnp.dot(yg_buf[...], wo[layer], preferred_element_type=jnp.float32).astype(jnp.bfloat16)
         o_copy(0, layer, q).start()
 
-    def stage_o(step, layer, q):
-        o_copy(step - 1, layer, q).wait()
-        mine = part[half_rows(q, core), :] if step == 1 else half_in2[0, q]
-        half_in2[step - 1, q] = (mine.astype(jnp.float32) + half_in[step - 1, q].astype(jnp.float32)).astype(jnp.bfloat16)
-        o_copy(step, layer, q).start()
+    def stage_half(layer, q):
+        o_copy(0, layer, q).wait()
+        mine = half_rows(q, core)
+        part[mine, :] = (part[mine, :].astype(jnp.float32) + half_in[q].astype(jnp.float32)).astype(jnp.bfloat16)
+        o_copy(1, layer, q).start()
+
+    def stage_quart(layer, q):
+        o_copy(1, layer, q).wait()
+        mine = part[quart_rows(q, core, bit_a), :]
+        quart_sum[q] = (mine.astype(jnp.float32) + quart_in[q].astype(jnp.float32)).astype(jnp.bfloat16)
+        o_copy(2, layer, q).start()
 
     def stage_own(layer, q):
         o_copy(2, layer, q).wait()
-        mine = half_rows(q, core)
-
-        @pl.loop(0, half // 16)
-        def _(i):
-            sub = pl.ds(pl.multiple_of(i * 16, 16), 16)
-            dst = pl.ds(pl.multiple_of(q * chunk + core * half + i * 16, 16), 16)
-            o_val = half_in2[1, q, sub, :].astype(jnp.float32) + half_in[2, q, sub, :].astype(jnp.float32)
+        for i in range(quart // 16):
+            sub = pl.ds(i * 16, 16)
+            dst = pl.ds(pl.multiple_of(q * chunk + core * half + bit_a * quart + i * 16, 16), 16)
+            o_val = quart_sum[q, sub, :].astype(jnp.float32) + pair_in[q, sub, :].astype(jnp.float32)
             if layer == 0:
                 o_acc[q, sub, :] = o_val
                 r = res[dst, :] + o_val
                 hid[dst, :] = (r * rms_scale(r, 1e-5) * norm_w[1:2, :].astype(jnp.float32)).astype(jnp.bfloat16)
             else:
                 hid[dst, :] = (o_acc[q, sub, :] + o_val).astype(jnp.bfloat16)
-
-        h_copy(layer, q).start()
+        h_copy(0, layer, q).start()
+        h_copy(1, layer, q).start()
+
+    def stage_forward(layer, q):
+        h_copy(0, layer, q).wait()
+        h_copy(2, layer, q).start()
 
     def stage_out(q):
-        h_copy(layers - 1, q).wait()
+        h_copy(1, layers - 1, q).wait()
+        h_copy(2, layers - 1, q).wait()
         rows = rows_of(q)
         r_out[rows, :] = res[rows, :] + hid[rows, :].astype(jnp.float32)
 
@@ -301,18 +324,20 @@
         stages.append(functools.partial(stage_in, layer))
         stages.append(functools.partial(stage_p, layer))
         stages.append(functools.partial(stage_ssm, layer))
-        stages.append(functools.partial(stage_o, 1, layer))
-        stages.append(functools.partial(stage_o, 2, layer))
+        stages.append(functools.partial(stage_half, layer))
+        stages.append(functools.partial(stage_quart, layer))
         stages.append(functools.partial(stage_own, layer))
+        stages.append(functools.partial(stage_forward, layer))
     stages.append(stage_out)
 
+    per_layer = len(stages) // layers
     progress = [0] * CHUNKS
+    second_ready = False
     fills = 0
     for q in ORDER:
         if q == CHUNKS:
             if fills == 0:
-                for tile in range(lane_tiles):
-                    w_load(1, tile).wait()
+                w_load(1).wait()
                 for row in range(3):
                     conv_load(1, row).start()
                 wo_load(1).start()
@@ -321,20 +346,21 @@
             split_weights(1, fills * split_step, split_step)
             fills += 1
         else:
-            if q == ORDER_FIRST[0] and progress[q] == 6:
+            if progress[q] == per_layer and not second_ready:
                 for row in range(3):
                     conv_load(1, row).wait()
+                second_ready = True
             stages[progress[q]](q)
             progress[q] += 1
 
 
 def dump_kernel(r_val, conv_val, ssm0, ssm1, r_hbm, conv_hbm, ssm_hbm, sems):
-    copies = [
-        pltpu.make_async_copy(ssm0, ssm_hbm.at[0], sems.at[0]),
-        pltpu.make_async_copy(ssm1, ssm_hbm.at[1], sems.at[1]),
-        pltpu.make_async_copy(conv_val, conv_hbm, sems.at[2]),
-        pltpu.make_async_copy(r_val, r_hbm, sems.at[3]),
-    ]
+    copies = [pltpu.make_async_copy(r_val, r_hbm, sems.at[0]), pltpu.make_async_copy(conv_val, conv_hbm, sems.at[1])]
+    piece = ssm0.shape[0] // DUMP_PIECES
+    for i in range(DUMP_PIECES):
+        for layer, ssm in enumerate((ssm0, ssm1)):
+            rows = pl.ds(i * piece, piece)
+            copies.append(pltpu.make_async_copy(ssm.at[rows], ssm_hbm.at[layer, rows], sems.at[2 + 2 * i + layer]))
     for copy in copies:
         copy.start()
     for copy in copies:
@@ -349,7 +375,9 @@
         lane_tiles = inner // 128
         chunk = tokens // CHUNKS
         half = chunk // 2
+        quart = chunk // 4
         w_view = w_in.reshape(2, width, 2, lane_tiles, 128).transpose(0, 1, 3, 2, 4)
+        w_view = with_layout_constraint(w_view, Layout(major_to_minor=(0, 1, 2, 3, 4))).reshape(2, width * 2 * lane_tiles, 128)
         conv_view = conv_state.transpose(0, 2, 1, 3)
         vmem = pl.BlockSpec(memory_space=pltpu.VMEM)
         anywhere = pl.BlockSpec(memory_space=pl.ANY)
@@ -368,7 +396,7 @@
             out_specs=[vmem] * 4,
             scratch_shapes=[
                 pltpu.VMEM((tokens, width), f32),
-                pltpu.VMEM((2, lane_tiles, width, 2, 128), bf16),
+                pltpu.VMEM((2, width * 2 * lane_tiles, 128), bf16),
                 pltpu.VMEM((2, width, 2 * inner), bf16),
                 pltpu.VMEM((2, inner, width), bf16),
                 pltpu.VMEM((2, tokens, inner), bf16),
@@ -384,19 +412,22 @@
                 pltpu.VMEM((tokens, inner), bf16),
                 pltpu.VMEM((tokens, inner), bf16),
                 pltpu.VMEM((tokens, width), bf16),
-                pltpu.VMEM((3, CHUNKS, half, width), bf16),
-                pltpu.VMEM((2, CHUNKS, half, width), bf16),
-                pltpu.VMEM((CHUNKS, half, width), f32),
+                pltpu.VMEM((CHUNKS, half, width), bf16),
+                pltpu.VMEM((CHUNKS, half // 2, width), bf16),
+                pltpu.VMEM((CHUNKS, half // 2, width), bf16),
+                pltpu.VMEM((CHUNKS, half // 2, width), bf16),
+                pltpu.VMEM((CHUNKS, half // 2, width), f32),
                 pltpu.VMEM((tokens, 128), f32),
                 pltpu.VMEM((2, tokens, 128), bf16),
                 pltpu.VMEM((4, tokens, 128), bf16),
+                pltpu.VMEM((state, inner), f32),
                 pltpu.VMEM((chunk, inner), f32),
                 pltpu.VMEM((chunk, inner), f32),
                 pltpu.VMEM((lane_tiles, chunk * 8, 128), f32),
                 pltpu.VMEM((chunk, inner), bf16),
                 pltpu.SemaphoreType.DMA((KINDS, 2, CHUNKS)),
                 pltpu.SemaphoreType.DMA((KINDS, 2, CHUNKS)),
-                pltpu.SemaphoreType.DMA((18,)),
+                pltpu.SemaphoreType.DMA((18 + CHUNKS,)),
                 pltpu.SemaphoreType.DMA((8,)),
                 pltpu.SemaphoreType.DMA((2, CHUNKS)),
             ],
@@ -412,7 +443,7 @@
             ],
             in_specs=[anywhere] * 4,
             out_specs=[hbm] * 3,
-            scratch_shapes=[pltpu.SemaphoreType.DMA((4,))],
+            scratch_shapes=[pltpu.SemaphoreType.DMA((2 + 2 * DUMP_PIECES,))],
             compiler_params=pltpu.CompilerParams(vmem_limit_bytes=2**20),
         )(r_val, conv_val, s0, s1)
         return r_new, conv_new.transpose(0, 2, 1, 3), ssm_new

time: 78.9 us -> 74.7 us (0.947)
  Pallas kernels: 78.1 us -> 73.8 us
    pallas_call x1, Pallas kernels: 67.7 us -> 63.6 us  [device_step(): pl.pallas_call(mamba_kernel, name='mamba', out_shape=[pltpu.VMEM((tokens,...]
where the time goes in v3:
time: 74.7 us; the launch traced here: 74.6 us
  Pallas kernels  73.8 us (99%)
  between operations  0.8 us (1%)
    pallas_call x1, Pallas kernels, device_step(): pl.pallas_call(mamba_kernel, name='mamba', out_shape=[pltpu.VMEM((tokens,...  63.6 us
    pallas_call x1, Pallas kernels, device_step(): pl.pallas_call(dump_kernel, name='dump', out_shape=[jax.ShapeDtypeStruct(...  10.2 us

profile of v3, /device:TPU:0, one launch (start us, length us, event | category | flops | bytes accessed | tf_op | source)
XLA Modules:
  0.0 74.6 jit_solution(15942415513518953748)
XLA Ops:
  0.6 63.6 %mamba.1 = (f32[512,1536]{1,0:T(8,128)S(1)}, bf16[2,3,512,384]{3,2,1,0:T(8,128)(2,1)S(1)}, f32[512,16,384]{2,1,0:T(8,128)S(1)}, f32[512,16,384]{2,1,0:T(8,128)S(1)}) custom-call(f32[512,1536]{1,0:T(8,128)} %residual.1, bf16[2,9216,128]{2,1,0:T(8,128)(2,1)} %bitcast.7, bf16[2,384,1536]{2,1,0:T(8,128)(2,1)} %w_out.1, bf16[2,3,512,384]{3,2,1,0:T(8,128)(2,1)} %bitcast.8, ...), custom_call_target="tpu_custom_call" | custom-call | tf_op jit(solution)/shard_map/mamba/pallas_call | solution.py:386
  64.2 10.2 %dump.1 = (f32[512,1536]{1,0:T(8,128)}, bf16[2,3,512,384]{3,2,1,0:T(8,128)(2,1)}, f32[2,512,16,384]{3,2,1,0:T(8,128)}) custom-call(f32[512,1536]{1,0:T(8,128)S(1)} %get-tuple-element.10.r_val, bf16[2,3,512,384]{3,2,1,0:T(8,128)(2,1)S(1)} %get-tuple-element.11.conv_val, f32[512,16,384]{2,1,0:T(8,128)S(1)} %get-tuple-element.12.ssm0, ...), custom_call_target="tpu_custom_call" | custom-call | tf_op jit(solution)/shard_map/dump/pallas_call | solution.py:436

commit v4 on v3

--- a/solution.py
+++ b/solution.py
@@ -10,13 +10,14 @@
 
 MESH = pl.DeviceIdType.MESH
 LOG2E = 1.4426950408889634
-CHUNKS = 4
+CHUNKS = 8
 KINDS = 10
-ORDER = (0, 2, 1, 0, 1, 3, 4, 4, 2, 4, 3, 0, 1, 2, 0, 1, 3, 2, 3, 0, 1, 2, 3, 0, 1, 2, 0, 3, 1, 0, 1, 2, 0, 3, 1, 2, 3, 2, 3, 0, 1, 2, 0, 1, 3, 2, 3, 0, 1, 2, 3, 0, 1, 2, 3, 0, 1, 2, 1, 3, 0, 2, 3)
-
+OFFSETS = ((0, 0, 2, 7, 9, 13, 17, 21), (23, 23, 25, 30, 32, 37, 45, 52))
+LAST_OFFSET = 55
+SPLIT_OFFSET = 17
 GROUP = 64
 DUMP_PIECES = 4
-ORDER_FIRST = tuple(dict.fromkeys(q for q in ORDER if q < CHUNKS))
+SPLIT_STEP = 4
 
 
 def rms_scale(vector, epsilon):
@@ -57,7 +58,7 @@
         pl.semaphore_signal(barrier, inc=1, device_id={"tp": peer}, device_id_type=MESH)
 
     def rows_of(q):
-        return pl.ds(q * chunk, chunk)
+        return pl.ds(pl.multiple_of(q * chunk, chunk), chunk)
 
     def half_rows(q, which):
         return pl.ds(pl.multiple_of(q * chunk + which * half, half), half)
@@ -113,11 +114,10 @@
         pltpu.make_async_copy(d_skip_hbm, d_skip, small_sem.at[7]),
     ]
     small[0].start()
-    res_load(ORDER[0]).start()
+    res_load(0).start()
     w_load(0).start()
-    for q in range(CHUNKS):
-        if q != ORDER[0]:
-            res_load(q).start()
+    for q in range(1, CHUNKS):
+        res_load(q).start()
     for row in range(3):
         conv_load(0, row).start()
     for copy in small[1:]:
@@ -136,10 +136,10 @@
         want = lax.rem(row, span) * (2 * lane_tiles) + lax.rem(group, lane_tiles) * 2 + lax.div(group, lane_tiles)
         pick = jnp.where(col == want, 1.0, 0.0).astype(jnp.bfloat16)
 
-        @pl.loop(0, count // 4)
+        @pl.loop(0, count // SPLIT_STEP)
         def _(step):
-            for i in range(4):
-                block = first + step * 4 + i
+            for i in range(SPLIT_STEP):
+                block = first + step * SPLIT_STEP + i
                 raw = [w_raw[layer, pl.ds(pl.multiple_of((2 * block + k) * packed, packed), packed), :] for k in range(2)]
                 both = jnp.dot(pick, jnp.concatenate(raw, axis=1), preferred_element_type=jnp.float32).astype(jnp.bfloat16)
                 for k in range(2):
@@ -147,8 +147,6 @@
                     for tile in range(2 * lane_tiles):
                         w_xz[layer, dst, tile * 128:(tile + 1) * 128] = both[tile * span:(tile + 1) * span, k * 128:(k + 1) * 128]
 
-    split_step = 8
-
     def first_norm(q):
         res_load(q).wait()
 
@@ -159,13 +157,13 @@
             hid[sub, :] = (r * rms_scale(r, 1e-5) * norm_w[0:1, :].astype(jnp.float32)).astype(jnp.bfloat16)
 
     small[0].wait()
-    first_norm(ORDER[0])
+    first_norm(0)
     w_load(0).wait()
 
     split_weights(0, 0, blocks)
 
     w_load(1).start()
-    for q in ORDER_FIRST:
+    for q in range(CHUNKS):
         state_load(0, q).start()
     wo_load(0).start()
     for row in range(3):
@@ -174,19 +172,22 @@
         copy.wait()
     pl.semaphore_wait(barrier, 4)
 
-    wo_ready = [False] * layers
-
     def stage_in(layer, q):
         rows = rows_of(q)
         if layer == 0:
-            if q != ORDER[0]:
+            @pl.when(q > 0)
+            def _():
                 first_norm(q)
         else:
             h_copy(1, layer - 1, q).wait()
             h_copy(2, layer - 1, q).wait()
-        xz = jnp.dot(hid[rows, :], w_xz[layer], preferred_element_type=jnp.float32)
-        x_val = xz[:, :inner].astype(jnp.bfloat16)
-        z_buf[rows, :] = xz[:, inner:].astype(jnp.bfloat16)
+
+            @pl.when(q == 0)
+            def _():
+                for row in range(3):
+                    conv_load(1, row).wait()
+
+        x_val = jnp.dot(hid[rows, :], w_xz[layer, :, :inner], preferred_element_type=jnp.float32).astype(jnp.bfloat16)
         conv_out[layer, 2, rows, :] = x_val
         taps = conv_w[layer].astype(jnp.float32)
         pre = conv_old[layer, rows, :].astype(jnp.float32) * taps[0:1]
@@ -200,6 +201,11 @@
         p_acc[rows, :] = p
         p_send[0, rows, :] = p.astype(jnp.bfloat16)
         p_copy(0, layer, q).start()
+
+    def stage_z(layer, q):
+        rows = rows_of(q)
+        z = jnp.dot(hid[rows, :], w_xz[layer, :, inner:], preferred_element_type=jnp.float32).astype(jnp.bfloat16).astype(jnp.float32)
+        z_buf[rows, :] = z * jax.nn.sigmoid(z)
 
     def stage_p(layer, q):
         rows = rows_of(q)
@@ -245,6 +251,7 @@
             b_now, c_now = carry
             for j in range(GROUP):
                 token = g * GROUP + j
+                y_rows = pl.ds(token * 8, 8) if chunk == GROUP else pl.ds(pl.multiple_of(token * 8, 8), 8)
                 dt_row = dt_buf[pl.ds(token, 1), :]
                 dx_row = dx_buf[pl.ds(token, 1), :]
                 old = state_buf[q * chunk + token]
@@ -253,32 +260,35 @@
                 weighted = new * c_now[:, j:j + 1]
                 partial = weighted[:8] + weighted[8:]
                 for tile in range(lane_tiles):
-                    y_part[tile, pl.ds(pl.multiple_of(token * 8, 8), 8), :] = partial[:, tile * 128:(tile + 1) * 128]
+                    y_part[tile, y_rows, :] = partial[:, tile * 128:(tile + 1) * 128]
             return pltpu.roll(b_now, 128 - GROUP, 1), pltpu.roll(c_now, 128 - GROUP, 1)
 
-        lax.fori_loop(0, chunk // GROUP, scan_group, (b_cols, c_cols))
-
-        @pl.loop(0, chunk // 32)
+        if chunk == GROUP:
+            scan_group(0, (b_cols, c_cols))
+        else:
+            lax.fori_loop(0, chunk // GROUP, scan_group, (b_cols, c_cols))
+
+        @pl.loop(0, chunk // 16)
         def _(g):
-            for k in range(4):
-                first = g * 256 + k * 64
+            halves = []
+            for k in range(2):
+                first = g * 128 + k * 64
                 by_tile = []
                 for tile in range(lane_tiles):
                     terms = [y_part[tile, pl.ds(first + sub, 8, stride=8), :] for sub in range(8)]
                     while len(terms) > 1:
                         terms = [terms[i] + terms[i + 1] for i in range(0, len(terms), 2)]
                     by_tile.append(terms[0])
-                y_buf_rows = pl.ds(pl.multiple_of(g * 32 + k * 8, 8), 8)
-                dt_buf[y_buf_rows, :] = jnp.concatenate(by_tile, axis=1)
-            sub = pl.ds(pl.multiple_of(g * 32, 32), 32)
-            sub_rows = pl.ds(pl.multiple_of(q * chunk + g * 32, 32), 32)
-            y = dt_buf[sub, :] + d_skip[layer:layer + 1, :] * xc_buf[sub_rows, :].astype(jnp.float32)
-            z = z_buf[sub_rows, :].astype(jnp.float32)
-            yg_buf[sub, :] = (y * (z * jax.nn.sigmoid(z))).astype(jnp.bfloat16)
-
-        if not wo_ready[layer]:
+                halves.append(jnp.concatenate(by_tile, axis=1))
+            sub = pl.ds(pl.multiple_of(g * 16, 16), 16)
+            sub_rows = pl.ds(pl.multiple_of(q * chunk + g * 16, 16), 16)
+            y = jnp.concatenate(halves, axis=0) + d_skip[layer:layer + 1, :] * xc_buf[sub_rows, :].astype(jnp.float32)
+            yg_buf[sub, :] = (y * z_buf[sub_rows, :]).astype(jnp.bfloat16)
+
+        @pl.when(q == 0)
+        def _():
             wo_load(layer).wait()
-            wo_ready[layer] = True
+
         part[rows, :] = jnp.dot(yg_buf[...], wo[layer], preferred_element_type=jnp.float32).astype(jnp.bfloat16)
         o_copy(0, layer, q).start()
 
@@ -319,39 +329,39 @@
         rows = rows_of(q)
         r_out[rows, :] = res[rows, :] + hid[rows, :].astype(jnp.float32)
 
-    stages = []
-    for layer in range(layers):
-        stages.append(functools.partial(stage_in, layer))
-        stages.append(functools.partial(stage_p, layer))
-        stages.append(functools.partial(stage_ssm, layer))
-        stages.append(functools.partial(stage_half, layer))
-        stages.append(functools.partial(stage_quart, layer))
-        stages.append(functools.partial(stage_own, layer))
-        stages.append(functools.partial(stage_forward, layer))
-    stages.append(stage_out)
-
-    per_layer = len(stages) // layers
-    progress = [0] * CHUNKS
-    second_ready = False
-    fills = 0
-    for q in ORDER:
-        if q == CHUNKS:
-            if fills == 0:
-                w_load(1).wait()
-                for row in range(3):
-                    conv_load(1, row).start()
-                wo_load(1).start()
-                for chunk_index in ORDER_FIRST:
-                    state_load(1, chunk_index).start()
-            split_weights(1, fills * split_step, split_step)
-            fills += 1
-        else:
-            if progress[q] == per_layer and not second_ready:
-                for row in range(3):
-                    conv_load(1, row).wait()
-                second_ready = True
-            stages[progress[q]](q)
-            progress[q] += 1
+    def stage_split(step):
+        @pl.when(step == 0)
+        def _():
+            w_load(1).wait()
+            for row in range(3):
+                conv_load(1, row).start()
+            wo_load(1).start()
+            for q in range(CHUNKS):
+                state_load(1, q).start()
+
+        split_weights(1, step * SPLIT_STEP, SPLIT_STEP)
+
+    stages = (stage_in, stage_z, stage_p, stage_ssm, stage_half, stage_quart, stage_own, stage_forward)
+    splits = blocks // SPLIT_STEP
+
+    def when_in(tick, offset, count, work):
+        @pl.when(jnp.logical_and(tick >= offset, tick < offset + count))
+        def _():
+            work(tick - offset)
+
+    @pl.loop(0, LAST_OFFSET + CHUNKS)
+    def _(tick):
+        for layer in range(layers):
+            def layer_stages(_, layer=layer):
+                for stage, offset in zip(stages, OFFSETS[layer]):
+                    when_in(tick, offset, CHUNKS, functools.partial(stage, layer))
+                if layer == 0:
+                    when_in(tick, SPLIT_OFFSET, splits, stage_split)
+                else:
+                    when_in(tick, LAST_OFFSET, CHUNKS, stage_out)
+
+            first, last = OFFSETS[layer][0], max(OFFSETS[layer][-1], LAST_OFFSET if layer else SPLIT_OFFSET)
+            when_in(tick, first, last + CHUNKS - first, layer_stages)
 
 
 def dump_kernel(r_val, conv_val, ssm0, ssm1, r_hbm, conv_hbm, ssm_hbm, sems):
@@ -410,7 +420,7 @@
                 pltpu.VMEM(d_skip.shape, f32),
                 pltpu.VMEM((tokens, width), bf16),
                 pltpu.VMEM((tokens, inner), bf16),
-                pltpu.VMEM((tokens, inner), bf16),
+                pltpu.VMEM((tokens, inner), f32),
                 pltpu.VMEM((tokens, width), bf16),
                 pltpu.VMEM((CHUNKS, half, width), bf16),
                 pltpu.VMEM((CHUNKS, half // 2, width), bf16),

time: 74.7 us -> 80.6 us (1.079)
  Pallas kernels: 73.8 us -> 79.8 us
    pallas_call x1, Pallas kernels: 63.6 us -> 69.6 us  [device_step(): pl.pallas_call(mamba_kernel, name='mamba', out_shape=[pltpu.VMEM((tokens,...]
where the time goes in v4:
time: 80.6 us; the launch traced here: 80.5 us
  Pallas kernels  79.8 us (99%)
    pallas_call x1, Pallas kernels, device_step(): pl.pallas_call(mamba_kernel, name='mamba', out_shape=[pltpu.VMEM((tokens,...  69.6 us
    pallas_call x1, Pallas kernels, device_step(): pl.pallas_call(dump_kernel, name='dump', out_shape=[jax.ShapeDtypeStruct(...  10.2 us

profile of v4, /device:TPU:0, one launch (start us, length us, event | category | flops | bytes accessed | tf_op | source)
XLA Modules:
  0.0 80.5 jit_solution(9030336537909013342)
XLA Ops:
  0.6 69.6 %mamba.1 = (f32[512,1536]{1,0:T(8,128)S(1)}, bf16[2,3,512,384]{3,2,1,0:T(8,128)(2,1)S(1)}, f32[512,16,384]{2,1,0:T(8,128)S(1)}, f32[512,16,384]{2,1,0:T(8,128)S(1)}) custom-call(f32[512,1536]{1,0:T(8,128)} %residual.1, bf16[2,9216,128]{2,1,0:T(8,128)(2,1)} %bitcast.7, bf16[2,384,1536]{2,1,0:T(8,128)(2,1)} %w_out.1, bf16[2,3,512,384]{3,2,1,0:T(8,128)(2,1)} %bitcast.8, ...), custom_call_target="tpu_custom_call" | custom-call | tf_op jit(solution)/shard_map/mamba/pallas_call | solution.py:396
  70.3 10.2 %dump.1 = (f32[512,1536]{1,0:T(8,128)}, bf16[2,3,512,384]{3,2,1,0:T(8,128)(2,1)}, f32[2,512,16,384]{3,2,1,0:T(8,128)}) custom-call(f32[512,1536]{1,0:T(8,128)S(1)} %get-tuple-element.10.r_val, bf16[2,3,512,384]{3,2,1,0:T(8,128)(2,1)S(1)} %get-tuple-element.11.conv_val, f32[512,16,384]{2,1,0:T(8,128)S(1)} %get-tuple-element.12.ssm0, ...), custom_call_target="tpu_custom_call" | custom-call | tf_op jit(solution)/shard_map/dump/pallas_call | solution.py:446

commit v5 on v4

--- a/solution.py
+++ b/solution.py
@@ -10,11 +10,11 @@
 
 MESH = pl.DeviceIdType.MESH
 LOG2E = 1.4426950408889634
-CHUNKS = 8
+CHUNKS = 4
 KINDS = 10
-OFFSETS = ((0, 0, 2, 7, 9, 13, 17, 21), (23, 23, 25, 30, 32, 37, 45, 52))
-LAST_OFFSET = 55
-SPLIT_OFFSET = 17
+OFFSETS = ((0, 0, 1, 8, 10, 13, 16, 18), (19, 20, 20, 23, 25, 28, 31, 34))
+LAST_OFFSET = 35
+SPLIT_OFFSET = 2
 GROUP = 64
 DUMP_PIECES = 4
 SPLIT_STEP = 4

time: 80.6 us -> 81.5 us (1.011)
  Pallas kernels: 79.8 us -> 80.7 us
    pallas_call x1, Pallas kernels: 69.6 us -> 70.5 us  [device_step(): pl.pallas_call(mamba_kernel, name='mamba', out_shape=[pltpu.VMEM((tokens,...]
where the time goes in v5:
time: 81.5 us; the launch traced here: 81.3 us
  Pallas kernels  80.7 us (99%)
    pallas_call x1, Pallas kernels, device_step(): pl.pallas_call(mamba_kernel, name='mamba', out_shape=[pltpu.VMEM((tokens,...  70.5 us
    pallas_call x1, Pallas kernels, device_step(): pl.pallas_call(dump_kernel, name='dump', out_shape=[jax.ShapeDtypeStruct(...  10.2 us

profile of v5, /device:TPU:0, one launch (start us, length us, event | category | flops | bytes accessed | tf_op | source)
XLA Modules:
  0.0 81.3 jit_solution(6522534062224190007)
XLA Ops:
  0.6 70.5 %mamba.1 = (f32[512,1536]{1,0:T(8,128)S(1)}, bf16[2,3,512,384]{3,2,1,0:T(8,128)(2,1)S(1)}, f32[512,16,384]{2,1,0:T(8,128)S(1)}, f32[512,16,384]{2,1,0:T(8,128)S(1)}) custom-call(f32[512,1536]{1,0:T(8,128)} %residual.1, bf16[2,9216,128]{2,1,0:T(8,128)(2,1)} %bitcast.7, bf16[2,384,1536]{2,1,0:T(8,128)(2,1)} %w_out.1, bf16[2,3,512,384]{3,2,1,0:T(8,128)(2,1)} %bitcast.8, ...), custom_call_target="tpu_custom_call" | custom-call | tf_op jit(solution)/shard_map/mamba/pallas_call | solution.py:396
  71.1 10.2 %dump.1 = (f32[512,1536]{1,0:T(8,128)}, bf16[2,3,512,384]{3,2,1,0:T(8,128)(2,1)}, f32[2,512,16,384]{3,2,1,0:T(8,128)}) custom-call(f32[512,1536]{1,0:T(8,128)S(1)} %get-tuple-element.10.r_val, bf16[2,3,512,384]{3,2,1,0:T(8,128)(2,1)S(1)} %get-tuple-element.11.conv_val, f32[512,16,384]{2,1,0:T(8,128)S(1)} %get-tuple-element.12.ssm0, ...), custom_call_target="tpu_custom_call" | custom-call | tf_op jit(solution)/shard_map/dump/pallas_call | solution.py:446

commit v6 on v3

--- a/solution.py
+++ b/solution.py
@@ -10,11 +10,11 @@
 
 MESH = pl.DeviceIdType.MESH
 LOG2E = 1.4426950408889634
-CHUNKS = 4
+CHUNKS = 8
 KINDS = 10
-ORDER = (0, 2, 1, 0, 1, 3, 4, 4, 2, 4, 3, 0, 1, 2, 0, 1, 3, 2, 3, 0, 1, 2, 3, 0, 1, 2, 0, 3, 1, 0, 1, 2, 0, 3, 1, 2, 3, 2, 3, 0, 1, 2, 0, 1, 3, 2, 3, 0, 1, 2, 3, 0, 1, 2, 3, 0, 1, 2, 1, 3, 0, 2, 3)
-
-GROUP = 64
+ORDER = (0, 1, 0, 3, 7, 0, 1, 7, 2, 1, 3, 5, 3, 7, 4, 2, 6, 6, 4, 5, 8, 2, 5, 4, 8, 8, 6, 0, 1, 3, 0, 2, 1, 4, 3, 6, 2, 0, 4, 5, 1, 6, 7, 3, 5, 2, 0, 7, 1, 8, 8, 6, 4, 8, 5, 2, 0, 3, 7, 1, 0, 6, 4, 1, 5, 2, 1, 0, 0, 3, 7, 1, 2, 2, 6, 4, 3, 2, 5, 3, 6, 6, 4, 4, 3, 7, 0, 6, 5, 4, 1, 5, 7, 0, 5, 7, 2, 1, 7, 3, 6, 4, 3, 2, 1, 5, 6, 0, 7, 4, 5, 3, 7, 2, 6, 1, 4, 5, 7, 3, 2, 6, 0, 4, 1, 5, 7, 0, 4, 5, 2, 3, 6, 7, 4, 0, 1, 2, 5, 6, 3, 7)
+
+GROUP = 16
 DUMP_PIECES = 4
 ORDER_FIRST = tuple(dict.fromkeys(q for q in ORDER if q < CHUNKS))
 
@@ -147,7 +147,7 @@
                     for tile in range(2 * lane_tiles):
                         w_xz[layer, dst, tile * 128:(tile + 1) * 128] = both[tile * span:(tile + 1) * span, k * 128:(k + 1) * 128]
 
-    split_step = 8
+    split_step = 4
 
     def first_norm(q):
         res_load(q).wait()
@@ -184,9 +184,7 @@
         else:
             h_copy(1, layer - 1, q).wait()
             h_copy(2, layer - 1, q).wait()
-        xz = jnp.dot(hid[rows, :], w_xz[layer], preferred_element_type=jnp.float32)
-        x_val = xz[:, :inner].astype(jnp.bfloat16)
-        z_buf[rows, :] = xz[:, inner:].astype(jnp.bfloat16)
+        x_val = jnp.dot(hid[rows, :], w_xz[layer, :, :inner], preferred_element_type=jnp.float32).astype(jnp.bfloat16)
         conv_out[layer, 2, rows, :] = x_val
         taps = conv_w[layer].astype(jnp.float32)
         pre = conv_old[layer, rows, :].astype(jnp.float32) * taps[0:1]
@@ -200,6 +198,11 @@
         p_acc[rows, :] = p
         p_send[0, rows, :] = p.astype(jnp.bfloat16)
         p_copy(0, layer, q).start()
+
+    def stage_z(layer, q):
+        rows = rows_of(q)
+        z = jnp.dot(hid[rows, :], w_xz[layer, :, inner:], preferred_element_type=jnp.float32).astype(jnp.bfloat16).astype(jnp.float32)
+        z_buf[rows, :] = z * jax.nn.sigmoid(z)
 
     def stage_p(layer, q):
         rows = rows_of(q)
@@ -243,38 +246,38 @@
 
         def scan_group(g, carry):
             b_now, c_now = carry
+            first = pl.multiple_of(g * GROUP, GROUP)
+            states = state_buf.at[pl.ds(q * chunk + first, GROUP)]
+            dts = dt_buf.at[pl.ds(first, GROUP)]
+            dxs = dx_buf.at[pl.ds(first, GROUP)]
+            ys = [y_part.at[tile, pl.ds(pl.multiple_of(first * 8, 8 * GROUP), 8 * GROUP)] for tile in range(lane_tiles)]
             for j in range(GROUP):
-                token = g * GROUP + j
-                dt_row = dt_buf[pl.ds(token, 1), :]
-                dx_row = dx_buf[pl.ds(token, 1), :]
-                old = state_buf[q * chunk + token]
-                new = jnp.exp2(dt_row * rate_buf[...]) * old + dx_row * b_now[:, j:j + 1]
-                state_buf[q * chunk + token] = new
+                new = jnp.exp2(dts[j:j + 1] * rate_buf[...]) * states[j] + dxs[j:j + 1] * b_now[:, j:j + 1]
+                states[j] = new
                 weighted = new * c_now[:, j:j + 1]
                 partial = weighted[:8] + weighted[8:]
                 for tile in range(lane_tiles):
-                    y_part[tile, pl.ds(pl.multiple_of(token * 8, 8), 8), :] = partial[:, tile * 128:(tile + 1) * 128]
+                    ys[tile][j * 8:(j + 1) * 8] = partial[:, tile * 128:(tile + 1) * 128]
             return pltpu.roll(b_now, 128 - GROUP, 1), pltpu.roll(c_now, 128 - GROUP, 1)
 
         lax.fori_loop(0, chunk // GROUP, scan_group, (b_cols, c_cols))
 
-        @pl.loop(0, chunk // 32)
+        @pl.loop(0, chunk // 16)
         def _(g):
-            for k in range(4):
-                first = g * 256 + k * 64
+            halves = []
+            for k in range(2):
+                first = g * 128 + k * 64
                 by_tile = []
                 for tile in range(lane_tiles):
-                    terms = [y_part[tile, pl.ds(first + sub, 8, stride=8), :] for sub in range(8)]
-                    while len(terms) > 1:
-                        terms = [terms[i] + terms[i + 1] for i in range(0, len(terms), 2)]
-                    by_tile.append(terms[0])
-                y_buf_rows = pl.ds(pl.multiple_of(g * 32 + k * 8, 8), 8)
-                dt_buf[y_buf_rows, :] = jnp.concatenate(by_tile, axis=1)
-            sub = pl.ds(pl.multiple_of(g * 32, 32), 32)
-            sub_rows = pl.ds(pl.multiple_of(q * chunk + g * 32, 32), 32)
-            y = dt_buf[sub, :] + d_skip[layer:layer + 1, :] * xc_buf[sub_rows, :].astype(jnp.float32)
-            z = z_buf[sub_rows, :].astype(jnp.float32)
-            yg_buf[sub, :] = (y * (z * jax.nn.sigmoid(z))).astype(jnp.bfloat16)
+                    total = y_part[tile, pl.ds(first, 8, stride=8), :]
+                    for step in range(1, 8):
+                        total = total + y_part[tile, pl.ds(first + step, 8, stride=8), :]
+                    by_tile.append(total)
+                halves.append(jnp.concatenate(by_tile, axis=1))
+            sub = pl.ds(pl.multiple_of(g * 16, 16), 16)
+            sub_rows = pl.ds(pl.multiple_of(q * chunk + g * 16, 16), 16)
+            y = jnp.concatenate(halves, axis=0) + d_skip[layer:layer + 1, :] * xc_buf[sub_rows, :].astype(jnp.float32)
+            yg_buf[sub, :] = (y * z_buf[sub_rows, :]).astype(jnp.bfloat16)
 
         if not wo_ready[layer]:
             wo_load(layer).wait()
@@ -322,6 +325,7 @@
     stages = []
     for layer in range(layers):
         stages.append(functools.partial(stage_in, layer))
+        stages.append(functools.partial(stage_z, layer))
         stages.append(functools.partial(stage_p, layer))
         stages.append(functools.partial(stage_ssm, layer))
         stages.append(functools.partial(stage_half, layer))
@@ -410,7 +414,7 @@
                 pltpu.VMEM(d_skip.shape, f32),
                 pltpu.VMEM((tokens, width), bf16),
                 pltpu.VMEM((tokens, inner), bf16),
-                pltpu.VMEM((tokens, inner), bf16),
+                pltpu.VMEM((tokens, inner), f32),
                 pltpu.VMEM((tokens, width), bf16),
                 pltpu.VMEM((CHUNKS, half, width), bf16),
                 pltpu.VMEM((CHUNKS, half // 2, width), bf16),

time: 74.7 us -> 81.2 us (1.087)
  Pallas kernels: 73.8 us -> 80.3 us
    pallas_call x1, Pallas kernels: 63.6 us -> 70.1 us  [device_step(): pl.pallas_call(mamba_kernel, name='mamba', out_shape=[pltpu.VMEM((tokens,...]
where the time goes in v6:
time: 81.2 us; the launch traced here: 81.1 us
  Pallas kernels  80.3 us (99%)
    pallas_call x1, Pallas kernels, device_step(): pl.pallas_call(mamba_kernel, name='mamba', out_shape=[pltpu.VMEM((tokens,...  70.1 us
    pallas_call x1, Pallas kernels, device_step(): pl.pallas_call(dump_kernel, name='dump', out_shape=[jax.ShapeDtypeStruct(...  10.2 us

profile of v6, /device:TPU:0, one launch (start us, length us, event | category | flops | bytes accessed | tf_op | source)
XLA Modules:
  0.0 81.1 jit_solution(4392949617417763098)
XLA Ops:
  0.6 70.1 %mamba.1 = (f32[512,1536]{1,0:T(8,128)S(1)}, bf16[2,3,512,384]{3,2,1,0:T(8,128)(2,1)S(1)}, f32[512,16,384]{2,1,0:T(8,128)S(1)}, f32[512,16,384]{2,1,0:T(8,128)S(1)}) custom-call(f32[512,1536]{1,0:T(8,128)} %residual.1, bf16[2,9216,128]{2,1,0:T(8,128)(2,1)} %bitcast.7, bf16[2,384,1536]{2,1,0:T(8,128)(2,1)} %w_out.1, bf16[2,3,512,384]{3,2,1,0:T(8,128)(2,1)} %bitcast.8, ...), custom_call_target="tpu_custom_call" | custom-call | tf_op jit(solution)/shard_map/mamba/pallas_call | solution.py:390
  70.7 10.2 %dump.1 = (f32[512,1536]{1,0:T(8,128)}, bf16[2,3,512,384]{3,2,1,0:T(8,128)(2,1)}, f32[2,512,16,384]{3,2,1,0:T(8,128)}) custom-call(f32[512,1536]{1,0:T(8,128)S(1)} %get-tuple-element.10.r_val, bf16[2,3,512,384]{3,2,1,0:T(8,128)(2,1)S(1)} %get-tuple-element.11.conv_val, f32[512,16,384]{2,1,0:T(8,128)S(1)} %get-tuple-element.12.ssm0, ...), custom_call_target="tpu_custom_call" | custom-call | tf_op jit(solution)/shard_map/dump/pallas_call | solution.py:440

commit v7 on v6

--- a/solution.py
+++ b/solution.py
@@ -10,11 +10,15 @@
 
 MESH = pl.DeviceIdType.MESH
 LOG2E = 1.4426950408889634
-CHUNKS = 8
+SIZES = (64, 128, 128, 128, 64)
+CHUNKS = len(SIZES)
+STARTS = tuple(sum(SIZES[:q]) for q in range(CHUNKS))
+LARGEST = max(SIZES)
 KINDS = 10
-ORDER = (0, 1, 0, 3, 7, 0, 1, 7, 2, 1, 3, 5, 3, 7, 4, 2, 6, 6, 4, 5, 8, 2, 5, 4, 8, 8, 6, 0, 1, 3, 0, 2, 1, 4, 3, 6, 2, 0, 4, 5, 1, 6, 7, 3, 5, 2, 0, 7, 1, 8, 8, 6, 4, 8, 5, 2, 0, 3, 7, 1, 0, 6, 4, 1, 5, 2, 1, 0, 0, 3, 7, 1, 2, 2, 6, 4, 3, 2, 5, 3, 6, 6, 4, 4, 3, 7, 0, 6, 5, 4, 1, 5, 7, 0, 5, 7, 2, 1, 7, 3, 6, 4, 3, 2, 1, 5, 6, 0, 7, 4, 5, 3, 7, 2, 6, 1, 4, 5, 7, 3, 2, 6, 0, 4, 1, 5, 7, 0, 4, 5, 2, 3, 6, 7, 4, 0, 1, 2, 5, 6, 3, 7)
-
-GROUP = 16
+ORDER = (0, 1, 0, 1, 5, 0, 2, 1, 3, 5, 5, 2, 4, 5, 5, 2, 4, 3, 3, 0, 1, 4, 0, 2, 1, 3, 0, 2, 5, 4, 3, 1, 0, 4, 2, 3, 1, 4, 0, 2, 0, 3, 1, 4, 1, 0, 2, 1, 0, 3, 1, 4, 2, 2, 3, 3, 2, 4, 0, 3, 4, 1, 4, 0, 2, 1, 3, 2, 0, 4, 3, 4, 1, 2, 3, 0, 4, 1, 2, 3, 4, 0, 1, 0, 2, 3, 4, 1, 2, 3, 4)
+
+W_PIECES = 3
+GROUP = 32
 DUMP_PIECES = 4
 ORDER_FIRST = tuple(dict.fromkeys(q for q in ORDER if q < CHUNKS))
 
@@ -31,9 +35,6 @@
 ):
     layers = 2
     tokens, width = res.shape
-    chunk = tokens // CHUNKS
-    half = chunk // 2
-    quart = chunk // 4
     inner = wo.shape[1]
     rank = w_dt_hbm.shape[1]
     state = a_log.shape[1]
@@ -57,13 +58,18 @@
         pl.semaphore_signal(barrier, inc=1, device_id={"tp": peer}, device_id_type=MESH)
 
     def rows_of(q):
-        return pl.ds(q * chunk, chunk)
+        return pl.ds(STARTS[q], SIZES[q])
 
     def half_rows(q, which):
-        return pl.ds(pl.multiple_of(q * chunk + which * half, half), half)
+        half = SIZES[q] // 2
+        return pl.ds(pl.multiple_of(STARTS[q] + which * half, half), half)
 
     def quart_rows(q, which_half, which):
-        return pl.ds(pl.multiple_of(q * chunk + which_half * half + which * quart, quart), quart)
+        quart = SIZES[q] // 4
+        return pl.ds(pl.multiple_of(STARTS[q] + which_half * (2 * quart) + which * quart, quart), quart)
+
+    def landing(ref, q, parts):
+        return ref.at[pl.ds(STARTS[q] // parts, SIZES[q] // parts)]
 
     def remote(kind, layer, q, src, dst, peer):
         return pltpu.make_async_remote_copy(
@@ -77,17 +83,18 @@
 
     def o_copy(step, layer, q):
         if step == 0:
-            return remote(4, layer, q, part.at[half_rows(q, 1 - core)], half_in.at[q], peer_c)
+            return remote(4, layer, q, part.at[half_rows(q, 1 - core)], landing(half_in, q, 2), peer_c)
         if step == 1:
-            return remote(5, layer, q, part.at[quart_rows(q, core, 1 - bit_a)], quart_in.at[q], peer_a)
-        return remote(6, layer, q, quart_sum.at[q], pair_in.at[q], peer_b)
+            return remote(5, layer, q, part.at[quart_rows(q, core, 1 - bit_a)], landing(quart_in, q, 4), peer_a)
+        return remote(6, layer, q, landing(quart_sum, q, 4), landing(pair_in, q, 4), peer_b)
 
     def h_copy(step, layer, q):
         ref = hid.at[quart_rows(q, core, 1 - bit_a if step == 2 else bit_a)]
         return remote(7 + step, layer, q, ref, ref, peer_a if step == 0 else peer_c)
 
-    def w_load(layer):
-        return pltpu.make_async_copy(w_in.at[layer], w_raw.at[layer], load_sem.at[layer])
+    def w_load(layer, piece):
+        rows = pl.ds(piece * (w_raw.shape[1] // W_PIECES), w_raw.shape[1] // W_PIECES)
+        return pltpu.make_async_copy(w_in.at[layer, rows], w_raw.at[layer, rows], load_sem.at[layer * W_PIECES + piece])
 
     def res_load(q):
         return pltpu.make_async_copy(residual.at[rows_of(q)], res.at[rows_of(q)], load_sem.at[18 + q])
@@ -114,7 +121,8 @@
     ]
     small[0].start()
     res_load(ORDER[0]).start()
-    w_load(0).start()
+    for piece in range(W_PIECES):
+        w_load(0, piece).start()
     for q in range(CHUNKS):
         if q != ORDER[0]:
             res_load(q).start()
@@ -152,19 +160,21 @@
     def first_norm(q):
         res_load(q).wait()
 
-        @pl.loop(0, chunk // 32)
+        @pl.loop(0, SIZES[q] // 32)
         def _(i):
-            sub = pl.ds(pl.multiple_of(q * chunk + i * 32, 32), 32)
+            sub = pl.ds(pl.multiple_of(STARTS[q] + i * 32, 32), 32)
             r = res[sub, :]
             hid[sub, :] = (r * rms_scale(r, 1e-5) * norm_w[0:1, :].astype(jnp.float32)).astype(jnp.bfloat16)
 
     small[0].wait()
     first_norm(ORDER[0])
-    w_load(0).wait()
-
-    split_weights(0, 0, blocks)
-
-    w_load(1).start()
+
+    for piece in range(W_PIECES):
+        w_load(0, piece).wait()
+        split_weights(0, piece * (blocks // W_PIECES), blocks // W_PIECES)
+
+    for piece in range(W_PIECES):
+        w_load(1, piece).start()
     for q in ORDER_FIRST:
         state_load(0, q).start()
     wo_load(0).start()
@@ -214,7 +224,7 @@
             p_copy(step, layer, q).start()
 
     def stage_ssm(layer, q):
-        rows = rows_of(q)
+        rows, start, chunk = rows_of(q), STARTS[q], SIZES[q]
         state_buf = ssm_bufs[layer]
         p = p_acc[rows, :]
         for step in (1, 2, 3):
@@ -236,8 +246,8 @@
         dt_low = jnp.where(is_dt, normed, 0.0).astype(jnp.bfloat16)
         pre = jnp.dot(dt_low, w_dt[layer], preferred_element_type=jnp.float32) + b_dt[layer:layer + 1, :]
         dt = jnp.maximum(pre, 0.0) + jnp.log1p(jnp.exp(-jnp.abs(pre)))
-        dt_buf[...] = dt
-        dx_buf[...] = dt * xc_buf[rows, :].astype(jnp.float32)
+        dt_buf[:chunk] = dt
+        dx_buf[:chunk] = dt * xc_buf[rows, :].astype(jnp.float32)
         turned = jnp.concatenate([normed] * (128 // chunk), axis=0).T
         b_cols = turned[rank:rank + state, :]
         c_cols = turned[rank + state:, :]
@@ -247,7 +257,7 @@
         def scan_group(g, carry):
             b_now, c_now = carry
             first = pl.multiple_of(g * GROUP, GROUP)
-            states = state_buf.at[pl.ds(q * chunk + first, GROUP)]
+            states = state_buf.at[pl.ds(start + first, GROUP)]
             dts = dt_buf.at[pl.ds(first, GROUP)]
             dxs = dx_buf.at[pl.ds(first, GROUP)]
             ys = [y_part.at[tile, pl.ds(pl.multiple_of(first * 8, 8 * GROUP), 8 * GROUP)] for tile in range(lane_tiles)]
@@ -275,40 +285,42 @@
                     by_tile.append(total)
                 halves.append(jnp.concatenate(by_tile, axis=1))
             sub = pl.ds(pl.multiple_of(g * 16, 16), 16)
-            sub_rows = pl.ds(pl.multiple_of(q * chunk + g * 16, 16), 16)
+            sub_rows = pl.ds(pl.multiple_of(start + g * 16, 16), 16)
             y = jnp.concatenate(halves, axis=0) + d_skip[layer:layer + 1, :] * xc_buf[sub_rows, :].astype(jnp.float32)
             yg_buf[sub, :] = (y * z_buf[sub_rows, :]).astype(jnp.bfloat16)
 
         if not wo_ready[layer]:
             wo_load(layer).wait()
             wo_ready[layer] = True
-        part[rows, :] = jnp.dot(yg_buf[...], wo[layer], preferred_element_type=jnp.float32).astype(jnp.bfloat16)
+        part[rows, :] = jnp.dot(yg_buf[:chunk], wo[layer], preferred_element_type=jnp.float32).astype(jnp.bfloat16)
         o_copy(0, layer, q).start()
 
     def stage_half(layer, q):
         o_copy(0, layer, q).wait()
         mine = half_rows(q, core)
-        part[mine, :] = (part[mine, :].astype(jnp.float32) + half_in[q].astype(jnp.float32)).astype(jnp.bfloat16)
+        part[mine, :] = (part[mine, :].astype(jnp.float32) + half_in[pl.ds(STARTS[q] // 2, SIZES[q] // 2), :].astype(jnp.float32)).astype(jnp.bfloat16)
         o_copy(1, layer, q).start()
 
     def stage_quart(layer, q):
         o_copy(1, layer, q).wait()
         mine = part[quart_rows(q, core, bit_a), :]
-        quart_sum[q] = (mine.astype(jnp.float32) + quart_in[q].astype(jnp.float32)).astype(jnp.bfloat16)
+        quarter = pl.ds(STARTS[q] // 4, SIZES[q] // 4)
+        quart_sum[quarter, :] = (mine.astype(jnp.float32) + quart_in[quarter, :].astype(jnp.float32)).astype(jnp.bfloat16)
         o_copy(2, layer, q).start()
 
     def stage_own(layer, q):
         o_copy(2, layer, q).wait()
+        quart = SIZES[q] // 4
         for i in range(quart // 16):
-            sub = pl.ds(i * 16, 16)
-            dst = pl.ds(pl.multiple_of(q * chunk + core * half + bit_a * quart + i * 16, 16), 16)
-            o_val = quart_sum[q, sub, :].astype(jnp.float32) + pair_in[q, sub, :].astype(jnp.float32)
+            sub = pl.ds(STARTS[q] // 4 + i * 16, 16)
+            dst = pl.ds(pl.multiple_of(STARTS[q] + core * (2 * quart) + bit_a * quart + i * 16, 16), 16)
+            o_val = quart_sum[sub, :].astype(jnp.float32) + pair_in[sub, :].astype(jnp.float32)
             if layer == 0:
-                o_acc[q, sub, :] = o_val
+                o_acc[sub, :] = o_val
                 r = res[dst, :] + o_val
                 hid[dst, :] = (r * rms_scale(r, 1e-5) * norm_w[1:2, :].astype(jnp.float32)).astype(jnp.bfloat16)
             else:
-                hid[dst, :] = (o_acc[q, sub, :] + o_val).astype(jnp.bfloat16)
+                hid[dst, :] = (o_acc[sub, :] + o_val).astype(jnp.bfloat16)
         h_copy(0, layer, q).start()
         h_copy(1, layer, q).start()
 
@@ -341,7 +353,8 @@
     for q in ORDER:
         if q == CHUNKS:
             if fills == 0:
-                w_load(1).wait()
+                for piece in range(W_PIECES):
+                    w_load(1, piece).wait()
                 for row in range(3):
                     conv_load(1, row).start()
                 wo_load(1).start()
@@ -377,9 +390,6 @@
         inner = w_out.shape[1]
         state = a_log.shape[1]
         lane_tiles = inner // 128
-        chunk = tokens // CHUNKS
-        half = chunk // 2
-        quart = chunk // 4
         w_view = w_in.reshape(2, width, 2, lane_tiles, 128).transpose(0, 1, 3, 2, 4)
         w_view = with_layout_constraint(w_view, Layout(major_to_minor=(0, 1, 2, 3, 4))).reshape(2, width * 2 * lane_tiles, 128)
         conv_view = conv_state.transpose(0, 2, 1, 3)
@@ -416,19 +426,19 @@
                 pltpu.VMEM((tokens, inner), bf16),
                 pltpu.VMEM((tokens, inner), f32),
                 pltpu.VMEM((tokens, width), bf16),
-                pltpu.VMEM((CHUNKS, half, width), bf16),
-                pltpu.VMEM((CHUNKS, half // 2, width), bf16),
-                pltpu.VMEM((CHUNKS, half // 2, width), bf16),
-                pltpu.VMEM((CHUNKS, half // 2, width), bf16),
-                pltpu.VMEM((CHUNKS, half // 2, width), f32),
+                pltpu.VMEM((tokens // 2, width), bf16),
+                pltpu.VMEM((tokens // 4, width), bf16),
+                pltpu.VMEM((tokens // 4, width), bf16),
+                pltpu.VMEM((tokens // 4, width), bf16),
+                pltpu.VMEM((tokens // 4, width), f32),
                 pltpu.VMEM((tokens, 128), f32),
                 pltpu.VMEM((2, tokens, 128), bf16),
                 pltpu.VMEM((4, tokens, 128), bf16),
                 pltpu.VMEM((state, inner), f32),
-                pltpu.VMEM((chunk, inner), f32),
-                pltpu.VMEM((chunk, inner), f32),
-                pltpu.VMEM((lane_tiles, chunk * 8, 128), f32),
-                pltpu.VMEM((chunk, inner), bf16),
+                pltpu.VMEM((LARGEST, inner), f32),
+                pltpu.VMEM((LARGEST, inner), f32),
+                pltpu.VMEM((lane_tiles, LARGEST * 8, 128), f32),
+                pltpu.VMEM((LARGEST, inner), bf16),
                 pltpu.SemaphoreType.DMA((KINDS, 2, CHUNKS)),
                 pltpu.SemaphoreType.DMA((KINDS, 2, CHUNKS)),
                 pltpu.SemaphoreType.DMA((18 + CHUNKS,)),

time: 81.2 us -> 75.8 us (0.933)
  Pallas kernels: 80.3 us -> 74.8 us
    pallas_call x1, Pallas kernels: 70.1 us -> 64.6 us  [device_step(): pl.pallas_call(mamba_kernel, name='mamba', out_shape=[pltpu.VMEM((tokens,...]
where the time goes in v7:
time: 75.8 us; the launch traced here: 75.6 us
  Pallas kernels  74.8 us (99%)
  between operations  0.8 us (1%)
    pallas_call x1, Pallas kernels, device_step(): pl.pallas_call(mamba_kernel, name='mamba', out_shape=[pltpu.VMEM((tokens,...  64.6 us
    pallas_call x1, Pallas kernels, device_step(): pl.pallas_call(dump_kernel, name='dump', out_shape=[jax.ShapeDtypeStruct(...  10.2 us

profile of v7, /device:TPU:0, one launch (start us, length us, event | category | flops | bytes accessed | tf_op | source)
XLA Modules:
  0.0 75.6 jit_solution(6804938454822002893)
XLA Ops:
  0.6 64.6 %mamba.1 = (f32[512,1536]{1,0:T(8,128)S(1)}, bf16[2,3,512,384]{3,2,1,0:T(8,128)(2,1)S(1)}, f32[512,16,384]{2,1,0:T(8,128)S(1)}, f32[512,16,384]{2,1,0:T(8,128)S(1)}) custom-call(f32[512,1536]{1,0:T(8,128)} %residual.1, bf16[2,9216,128]{2,1,0:T(8,128)(2,1)} %bitcast.7, bf16[2,384,1536]{2,1,0:T(8,128)(2,1)} %w_out.1, bf16[2,3,512,384]{3,2,1,0:T(8,128)(2,1)} %bitcast.8, ...), custom_call_target="tpu_custom_call" | custom-call | tf_op jit(solution)/shard_map/mamba/pallas_call | solution.py:400
  65.2 10.2 %dump.1 = (f32[512,1536]{1,0:T(8,128)}, bf16[2,3,512,384]{3,2,1,0:T(8,128)(2,1)}, f32[2,512,16,384]{3,2,1,0:T(8,128)}) custom-call(f32[512,1536]{1,0:T(8,128)S(1)} %get-tuple-element.10.r_val, bf16[2,3,512,384]{3,2,1,0:T(8,128)(2,1)S(1)} %get-tuple-element.11.conv_val, f32[512,16,384]{2,1,0:T(8,128)S(1)} %get-tuple-element.12.ssm0, ...), custom_call_target="tpu_custom_call" | custom-call | tf_op jit(solution)/shard_map/dump/pallas_call | solution.py:450

commit v8 on v7

--- a/solution.py
+++ b/solution.py
@@ -15,10 +15,10 @@
 STARTS = tuple(sum(SIZES[:q]) for q in range(CHUNKS))
 LARGEST = max(SIZES)
 KINDS = 10
-ORDER = (0, 1, 0, 1, 5, 0, 2, 1, 3, 5, 5, 2, 4, 5, 5, 2, 4, 3, 3, 0, 1, 4, 0, 2, 1, 3, 0, 2, 5, 4, 3, 1, 0, 4, 2, 3, 1, 4, 0, 2, 0, 3, 1, 4, 1, 0, 2, 1, 0, 3, 1, 4, 2, 2, 3, 3, 2, 4, 0, 3, 4, 1, 4, 0, 2, 1, 3, 2, 0, 4, 3, 4, 1, 2, 3, 0, 4, 1, 2, 3, 4, 0, 1, 0, 2, 3, 4, 1, 2, 3, 4)
+ORDER = (0, 1, 3, 0, 2, 1, 4, 2, 3, 0, 1, 4, 0, 2, 1, 3, 5, 0, 5, 2, 4, 3, 1, 5, 4, 5, 0, 5, 2, 3, 5, 1, 4, 0, 2, 3, 1, 0, 4, 1, 2, 0, 3, 1, 2, 3, 4, 2, 0, 4, 3, 1, 4, 0, 2, 1, 3, 2, 0, 4, 3, 4, 1, 2, 3, 0, 4, 1, 2, 3, 4, 1, 2, 3, 0, 4, 3, 0, 1, 2, 4)
 
 W_PIECES = 3
-GROUP = 32
+GROUPS = {64: 16, 128: 64}
 DUMP_PIECES = 4
 ORDER_FIRST = tuple(dict.fromkeys(q for q in ORDER if q < CHUNKS))
 
@@ -31,7 +31,7 @@
     residual, w_in, w_out, conv_state, ssm_state, norm_w_hbm, conv_w_hbm, conv_b_hbm, w_x_hbm, w_dt_hbm, b_dt_hbm, a_log_hbm, d_skip_hbm,
     r_out, conv_out, ssm0, ssm1,
     res, w_raw, w_xz, wo, conv_old, norm_w, conv_w, conv_b, w_x, w_dt, b_dt, a_log, d_skip, hid, xc_buf, z_buf, part, half_in, quart_in, quart_sum, pair_in, o_acc,
-    p_acc, p_send, p_recv, rate_buf, dt_buf, dx_buf, y_part, yg_buf, send_sem, recv_sem, load_sem, small_sem, state_sem,
+    p_acc, p_send, p_recv, dt_buf, dx_buf, y_part, yg_buf, send_sem, recv_sem, load_sem, small_sem, state_sem,
 ):
     layers = 2
     tokens, width = res.shape
@@ -194,7 +194,10 @@
         else:
             h_copy(1, layer - 1, q).wait()
             h_copy(2, layer - 1, q).wait()
-        x_val = jnp.dot(hid[rows, :], w_xz[layer, :, :inner], preferred_element_type=jnp.float32).astype(jnp.bfloat16)
+        xz = jnp.dot(hid[rows, :], w_xz[layer], preferred_element_type=jnp.float32).astype(jnp.bfloat16)
+        x_val = xz[:, :inner]
+        z = xz[:, inner:].astype(jnp.float32)
+        z_buf[rows, :] = z * jax.nn.sigmoid(z)
         conv_out[layer, 2, rows, :] = x_val
         taps = conv_w[layer].astype(jnp.float32)
         pre = conv_old[layer, rows, :].astype(jnp.float32) * taps[0:1]
@@ -209,11 +212,6 @@
         p_send[0, rows, :] = p.astype(jnp.bfloat16)
         p_copy(0, layer, q).start()
 
-    def stage_z(layer, q):
-        rows = rows_of(q)
-        z = jnp.dot(hid[rows, :], w_xz[layer, :, inner:], preferred_element_type=jnp.float32).astype(jnp.bfloat16).astype(jnp.float32)
-        z_buf[rows, :] = z * jax.nn.sigmoid(z)
-
     def stage_p(layer, q):
         rows = rows_of(q)
         p_copy(0, layer, q).wait()
@@ -251,26 +249,28 @@
         turned = jnp.concatenate([normed] * (128 // chunk), axis=0).T
         b_cols = turned[rank:rank + state, :]
         c_cols = turned[rank + state:, :]
-        rate_buf[...] = jnp.exp(a_log[layer]) * (-LOG2E)
         state_load(layer, q).wait()
+
+        group = GROUPS[chunk]
+        rate = jnp.exp(a_log[layer]) * (-LOG2E)
 
         def scan_group(g, carry):
             b_now, c_now = carry
-            first = pl.multiple_of(g * GROUP, GROUP)
-            states = state_buf.at[pl.ds(start + first, GROUP)]
-            dts = dt_buf.at[pl.ds(first, GROUP)]
-            dxs = dx_buf.at[pl.ds(first, GROUP)]
-            ys = [y_part.at[tile, pl.ds(pl.multiple_of(first * 8, 8 * GROUP), 8 * GROUP)] for tile in range(lane_tiles)]
-            for j in range(GROUP):
-                new = jnp.exp2(dts[j:j + 1] * rate_buf[...]) * states[j] + dxs[j:j + 1] * b_now[:, j:j + 1]
+            first = pl.multiple_of(g * group, group)
+            states = state_buf.at[pl.ds(start + first, group)]
+            dts = dt_buf.at[pl.ds(first, group)]
+            dxs = dx_buf.at[pl.ds(first, group)]
+            ys = [y_part.at[tile, pl.ds(pl.multiple_of(first * 8, 8 * group), 8 * group)] for tile in range(lane_tiles)]
+            for j in range(group):
+                new = jnp.exp2(dts[j:j + 1] * rate) * states[j] + dxs[j:j + 1] * b_now[:, j:j + 1]
                 states[j] = new
                 weighted = new * c_now[:, j:j + 1]
                 partial = weighted[:8] + weighted[8:]
                 for tile in range(lane_tiles):
                     ys[tile][j * 8:(j + 1) * 8] = partial[:, tile * 128:(tile + 1) * 128]
-            return pltpu.roll(b_now, 128 - GROUP, 1), pltpu.roll(c_now, 128 - GROUP, 1)
-
-        lax.fori_loop(0, chunk // GROUP, scan_group, (b_cols, c_cols))
+            return pltpu.roll(b_now, 128 - group, 1), pltpu.roll(c_now, 128 - group, 1)
+
+        lax.fori_loop(0, chunk // group, scan_group, (b_cols, c_cols))
 
         @pl.loop(0, chunk // 16)
         def _(g):
@@ -337,7 +337,6 @@
     stages = []
     for layer in range(layers):
         stages.append(functools.partial(stage_in, layer))
-        stages.append(functools.partial(stage_z, layer))
         stages.append(functools.partial(stage_p, layer))
         stages.append(functools.partial(stage_ssm, layer))
         stages.append(functools.partial(stage_half, layer))
@@ -434,7 +433,6 @@
                 pltpu.VMEM((tokens, 128), f32),
                 pltpu.VMEM((2, tokens, 128), bf16),
                 pltpu.VMEM((4, tokens, 128), bf16),
-                pltpu.VMEM((state, inner), f32),
                 pltpu.VMEM((LARGEST, inner), f32),
                 pltpu.VMEM((LARGEST, inner), f32),
                 pltpu.VMEM((lane_tiles, LARGEST * 8, 128), f32),

time: 75.8 us -> 73.5 us (0.970)
  Pallas kernels: 74.8 us -> 72.5 us
    pallas_call x1, Pallas kernels: 64.6 us -> 62.3 us  [device_step(): pl.pallas_call(mamba_kernel, name='mamba', out_shape=[pltpu.VMEM((tokens,...]
where the time goes in v8:
time: 73.5 us; the launch traced here: 73.3 us
  Pallas kernels  72.5 us (99%)
  between operations  0.8 us (1%)
    pallas_call x1, Pallas kernels, device_step(): pl.pallas_call(mamba_kernel, name='mamba', out_shape=[pltpu.VMEM((tokens,...  62.3 us
    pallas_call x1, Pallas kernels, device_step(): pl.pallas_call(dump_kernel, name='dump', out_shape=[jax.ShapeDtypeStruct(...  10.2 us

profile of v8, /device:TPU:0, one launch (start us, length us, event | category | flops | bytes accessed | tf_op | source)
XLA Modules:
  0.0 73.3 jit_solution(3240296838615324036)
XLA Ops:
  0.6 62.3 %mamba.1 = (f32[512,1536]{1,0:T(8,128)S(1)}, bf16[2,3,512,384]{3,2,1,0:T(8,128)(2,1)S(1)}, f32[512,16,384]{2,1,0:T(8,128)S(1)}, f32[512,16,384]{2,1,0:T(8,128)S(1)}) custom-call(f32[512,1536]{1,0:T(8,128)} %residual.1, bf16[2,9216,128]{2,1,0:T(8,128)(2,1)} %bitcast.7, bf16[2,384,1536]{2,1,0:T(8,128)(2,1)} %w_out.1, bf16[2,3,512,384]{3,2,1,0:T(8,128)(2,1)} %bitcast.8, ...), custom_call_target="tpu_custom_call" | custom-call | tf_op jit(solution)/shard_map/mamba/pallas_call | solution.py:399
  62.9 10.2 %dump.1 = (f32[512,1536]{1,0:T(8,128)}, bf16[2,3,512,384]{3,2,1,0:T(8,128)(2,1)}, f32[2,512,16,384]{3,2,1,0:T(8,128)}) custom-call(f32[512,1536]{1,0:T(8,128)S(1)} %get-tuple-element.10.r_val, bf16[2,3,512,384]{3,2,1,0:T(8,128)(2,1)S(1)} %get-tuple-element.11.conv_val, f32[512,16,384]{2,1,0:T(8,128)S(1)} %get-tuple-element.12.ssm0, ...), custom_call_target="tpu_custom_call" | custom-call | tf_op jit(solution)/shard_map/dump/pallas_call | solution.py:448

commit v9 on v8

--- a/solution.py
+++ b/solution.py
@@ -15,7 +15,7 @@
 STARTS = tuple(sum(SIZES[:q]) for q in range(CHUNKS))
 LARGEST = max(SIZES)
 KINDS = 10
-ORDER = (0, 1, 3, 0, 2, 1, 4, 2, 3, 0, 1, 4, 0, 2, 1, 3, 5, 0, 5, 2, 4, 3, 1, 5, 4, 5, 0, 5, 2, 3, 5, 1, 4, 0, 2, 3, 1, 0, 4, 1, 2, 0, 3, 1, 2, 3, 4, 2, 0, 4, 3, 1, 4, 0, 2, 1, 3, 2, 0, 4, 3, 4, 1, 2, 3, 0, 4, 1, 2, 3, 4, 1, 2, 3, 0, 4, 3, 0, 1, 2, 4)
+ORDER = (0, 1, 5, 2, 5, 0, 3, 1, 4, 2, 4, 3, 0, 1, 0, 2, 1, 3, 5, 2, 4, 0, 5, 3, 1, 4, 5, 2, 0, 3, 1, 4, 5, 0, 2, 3, 1, 0, 4, 1, 2, 0, 1, 3, 2, 4, 3, 2, 4, 0, 3, 1, 0, 4, 2, 1, 3, 2, 0, 4, 3, 1, 4, 2, 3, 4, 1, 0, 2, 3, 4, 1, 0, 2, 0, 1, 3, 4, 2, 3, 4)
 
 W_PIECES = 3
 GROUPS = {64: 16, 128: 64}
@@ -123,13 +123,6 @@
     res_load(ORDER[0]).start()
     for piece in range(W_PIECES):
         w_load(0, piece).start()
-    for q in range(CHUNKS):
-        if q != ORDER[0]:
-            res_load(q).start()
-    for row in range(3):
-        conv_load(0, row).start()
-    for copy in small[1:]:
-        copy.start()
     for layer in range(layers):
         w_dt[layer, rank:] = jnp.zeros((128 - rank, inner), jnp.bfloat16)
 
@@ -171,6 +164,13 @@
 
     for piece in range(W_PIECES):
         w_load(0, piece).wait()
+        if piece == 0:
+            for row in range(3):
+                conv_load(0, row).start()
+            for copy in small[1:]:
+                copy.start()
+            for q in ORDER_FIRST[1:]:
+                res_load(q).start()
         split_weights(0, piece * (blocks // W_PIECES), blocks // W_PIECES)
 
     for piece in range(W_PIECES):

time: 73.5 us -> 76.5 us (1.041)
  Pallas kernels: 72.5 us -> 75.5 us
    pallas_call x1, Pallas kernels: 62.3 us -> 65.3 us  [device_step(): pl.pallas_call(mamba_kernel, name='mamba', out_shape=[pltpu.VMEM((tokens,...]
where the time goes in v9:
time: 76.5 us; the launch traced here: 76.3 us
  Pallas kernels  75.5 us (99%)
  between operations  0.8 us (1%)
    pallas_call x1, Pallas kernels, device_step(): pl.pallas_call(mamba_kernel, name='mamba', out_shape=[pltpu.VMEM((tokens,...  65.3 us
    pallas_call x1, Pallas kernels, device_step(): pl.pallas_call(dump_kernel, name='dump', out_shape=[jax.ShapeDtypeStruct(...  10.2 us

profile of v9, /device:TPU:0, one launch (start us, length us, event | category | flops | bytes accessed | tf_op | source)
XLA Modules:
  0.0 76.3 jit_solution(15846657051328956083)
XLA Ops:
  0.6 65.3 %mamba.1 = (f32[512,1536]{1,0:T(8,128)S(1)}, bf16[2,3,512,384]{3,2,1,0:T(8,128)(2,1)S(1)}, f32[512,16,384]{2,1,0:T(8,128)S(1)}, f32[512,16,384]{2,1,0:T(8,128)S(1)}) custom-call(f32[512,1536]{1,0:T(8,128)} %residual.1, bf16[2,9216,128]{2,1,0:T(8,128)(2,1)} %bitcast.7, bf16[2,384,1536]{2,1,0:T(8,128)(2,1)} %w_out.1, bf16[2,3,512,384]{3,2,1,0:T(8,128)(2,1)} %bitcast.8, ...), custom_call_target="tpu_custom_call" | custom-call | tf_op jit(solution)/shard_map/mamba/pallas_call | solution.py:399
  66.0 10.2 %dump.1 = (f32[512,1536]{1,0:T(8,128)}, bf16[2,3,512,384]{3,2,1,0:T(8,128)(2,1)}, f32[2,512,16,384]{3,2,1,0:T(8,128)}) custom-call(f32[512,1536]{1,0:T(8,128)S(1)} %get-tuple-element.10.r_val, bf16[2,3,512,384]{3,2,1,0:T(8,128)(2,1)S(1)} %get-tuple-element.11.conv_val, f32[512,16,384]{2,1,0:T(8,128)S(1)} %get-tuple-element.12.ssm0, ...), custom_call_target="tpu_custom_call" | custom-call | tf_op jit(solution)/shard_map/dump/pallas_call | solution.py:448

commit v10 on v8

--- a/solution.py
+++ b/solution.py
@@ -123,9 +123,6 @@
     res_load(ORDER[0]).start()
     for piece in range(W_PIECES):
         w_load(0, piece).start()
-    for q in range(CHUNKS):
-        if q != ORDER[0]:
-            res_load(q).start()
     for row in range(3):
         conv_load(0, row).start()
     for copy in small[1:]:
@@ -171,6 +168,9 @@
 
     for piece in range(W_PIECES):
         w_load(0, piece).wait()
+        if piece == 0:
+            for q in ORDER_FIRST[1:]:
+                res_load(q).start()
         split_weights(0, piece * (blocks // W_PIECES), blocks // W_PIECES)
 
     for piece in range(W_PIECES):

time: 73.5 us -> 73.5 us (level)
  no operation moved by 1% of the time
where the time goes in v10:
time: 73.5 us; the launch traced here: 73.3 us
  Pallas kernels  72.5 us (99%)
  between operations  0.8 us (1%)
    pallas_call x1, Pallas kernels, device_step(): pl.pallas_call(mamba_kernel, name='mamba', out_shape=[pltpu.VMEM((tokens,...  62.3 us
    pallas_call x1, Pallas kernels, device_step(): pl.pallas_call(dump_kernel, name='dump', out_shape=[jax.ShapeDtypeStruct(...  10.2 us

profile of v10, /device:TPU:0, one launch (start us, length us, event | category | flops | bytes accessed | tf_op | source)
XLA Modules:
  0.0 73.3 jit_solution(13693129712248575282)
XLA Ops:
  0.6 62.3 %mamba.1 = (f32[512,1536]{1,0:T(8,128)S(1)}, bf16[2,3,512,384]{3,2,1,0:T(8,128)(2,1)S(1)}, f32[512,16,384]{2,1,0:T(8,128)S(1)}, f32[512,16,384]{2,1,0:T(8,128)S(1)}) custom-call(f32[512,1536]{1,0:T(8,128)} %residual.1, bf16[2,9216,128]{2,1,0:T(8,128)(2,1)} %bitcast.7, bf16[2,384,1536]{2,1,0:T(8,128)(2,1)} %w_out.1, bf16[2,3,512,384]{3,2,1,0:T(8,128)(2,1)} %bitcast.8, ...), custom_call_target="tpu_custom_call" | custom-call | tf_op jit(solution)/shard_map/mamba/pallas_call | solution.py:399
  63.0 10.2 %dump.1 = (f32[512,1536]{1,0:T(8,128)}, bf16[2,3,512,384]{3,2,1,0:T(8,128)(2,1)}, f32[2,512,16,384]{3,2,1,0:T(8,128)}) custom-call(f32[512,1536]{1,0:T(8,128)S(1)} %get-tuple-element.10.r_val, bf16[2,3,512,384]{3,2,1,0:T(8,128)(2,1)S(1)} %get-tuple-element.11.conv_val, f32[512,16,384]{2,1,0:T(8,128)S(1)} %get-tuple-element.12.ssm0, ...), custom_call_target="tpu_custom_call" | custom-call | tf_op jit(solution)/shard_map/dump/pallas_call | solution.py:448

commit v11 on v8

--- a/solution.py
+++ b/solution.py
@@ -15,7 +15,7 @@
 STARTS = tuple(sum(SIZES[:q]) for q in range(CHUNKS))
 LARGEST = max(SIZES)
 KINDS = 10
-ORDER = (0, 1, 3, 0, 2, 1, 4, 2, 3, 0, 1, 4, 0, 2, 1, 3, 5, 0, 5, 2, 4, 3, 1, 5, 4, 5, 0, 5, 2, 3, 5, 1, 4, 0, 2, 3, 1, 0, 4, 1, 2, 0, 3, 1, 2, 3, 4, 2, 0, 4, 3, 1, 4, 0, 2, 1, 3, 2, 0, 4, 3, 4, 1, 2, 3, 0, 4, 1, 2, 3, 4, 1, 2, 3, 0, 4, 3, 0, 1, 2, 4)
+ORDER = (0, 1, 0, 2, 1, 3, 5, 5, 5, 4, 2, 5, 3, 0, 1, 4, 0, 2, 1, 3, 5, 2, 0, 4, 3, 1, 5, 4, 2, 0, 3, 1, 4, 2, 0, 3, 1, 0, 4, 1, 0, 2, 3, 1, 2, 3, 4, 2, 0, 3, 4, 1, 4, 0, 2, 1, 3, 2, 0, 4, 3, 1, 4, 2, 3, 0, 4, 1, 2, 3, 4, 1, 2, 0, 3, 4, 3, 0, 1, 2, 4)
 
 W_PIECES = 3
 GROUPS = {64: 16, 128: 64}

time: 73.5 us -> 72.6 us (0.988)
  Pallas kernels: 72.5 us -> 71.6 us
    pallas_call x1, Pallas kernels: 62.3 us -> 61.4 us  [device_step(): pl.pallas_call(mamba_kernel, name='mamba', out_shape=[pltpu.VMEM((tokens,...]
where the time goes in v11:
time: 72.6 us; the launch traced here: 72.4 us
  Pallas kernels  71.6 us (99%)
  between operations  0.8 us (1%)
    pallas_call x1, Pallas kernels, device_step(): pl.pallas_call(mamba_kernel, name='mamba', out_shape=[pltpu.VMEM((tokens,...  61.4 us
    pallas_call x1, Pallas kernels, device_step(): pl.pallas_call(dump_kernel, name='dump', out_shape=[jax.ShapeDtypeStruct(...  10.2 us

profile of v11, /device:TPU:0, one launch (start us, length us, event | category | flops | bytes accessed | tf_op | source)
XLA Modules:
  0.0 72.4 jit_solution(12700961411312376281)
XLA Ops:
  0.6 61.4 %mamba.1 = (f32[512,1536]{1,0:T(8,128)S(1)}, bf16[2,3,512,384]{3,2,1,0:T(8,128)(2,1)S(1)}, f32[512,16,384]{2,1,0:T(8,128)S(1)}, f32[512,16,384]{2,1,0:T(8,128)S(1)}) custom-call(f32[512,1536]{1,0:T(8,128)} %residual.1, bf16[2,9216,128]{2,1,0:T(8,128)(2,1)} %bitcast.7, bf16[2,384,1536]{2,1,0:T(8,128)(2,1)} %w_out.1, bf16[2,3,512,384]{3,2,1,0:T(8,128)(2,1)} %bitcast.8, ...), custom_call_target="tpu_custom_call" | custom-call | tf_op jit(solution)/shard_map/mamba/pallas_call | solution.py:399
  62.1 10.2 %dump.1 = (f32[512,1536]{1,0:T(8,128)}, bf16[2,3,512,384]{3,2,1,0:T(8,128)(2,1)}, f32[2,512,16,384]{3,2,1,0:T(8,128)}) custom-call(f32[512,1536]{1,0:T(8,128)S(1)} %get-tuple-element.10.r_val, bf16[2,3,512,384]{3,2,1,0:T(8,128)(2,1)S(1)} %get-tuple-element.11.conv_val, f32[512,16,384]{2,1,0:T(8,128)S(1)} %get-tuple-element.12.ssm0, ...), custom_call_target="tpu_custom_call" | custom-call | tf_op jit(solution)/shard_map/dump/pallas_call | solution.py:448
